TPU v7x, 32 devices: a 4x4x1 block of a 4x4x8 slice. The times are simulated.
32 devices in a mesh: data: 1 (over z), dap: 32 (over y, x, core).
Axes of the slice: x: 4, y: 4, z: 1, core: 2. Of those that a mesh axis runs over, the one named last changes fastest.
The devices are a block of a 4x4x8 slice.
Arguments:
- msa_act: bfloat16 [256, 128, 384], P(('data', 'dap'))
- pair_act: bfloat16 [128, 128, 288], P(('data', 'dap'))
- msa_mask: int32 [256, 128], P('data')
- res_mask: int32 [128], P('data')
- w_row_bias: bfloat16 [2, 288, 12], replicated
- w_row_in: bfloat16 [2, 384, 4, 12, 32], replicated
- w_row_out: bfloat16 [2, 12, 32, 384], replicated
- w_col_in: bfloat16 [2, 384, 4, 12, 32], replicated
- w_col_out: bfloat16 [2, 12, 32, 384], replicated
- w_opm_in: bfloat16 [2, 384, 2, 32], replicated
- w_opm_out: bfloat16 [2, 32, 32, 288], replicated
- w_ts_bias: bfloat16 [2, 288, 8], replicated
- w_ts_in: bfloat16 [2, 288, 4, 8, 36], replicated
- w_ts_out: bfloat16 [2, 8, 36, 288], replicated
- w_te_bias: bfloat16 [2, 288, 8], replicated
- w_te_in: bfloat16 [2, 288, 4, 8, 36], replicated
- w_te_out: bfloat16 [2, 8, 36, 288], replicated
Outputs:
- output 1: bfloat16 [256, 128, 384], P(('data', 'dap'))
- output 2: bfloat16 [128, 128, 288], P(('data', 'dap'))
All inputs are finite; a program needn't handle non-finite values.
Results may differ from a plain program's by a relative error of at most 0.0173621.
Values are sent between devices in bfloat16 or wider.
A program may use at most 768 MiB of HBM per device.

v0:
```python
import jax
import jax.numpy as jnp
from jax import lax
from jax.sharding import PartitionSpec as P


def layer_norm(values):
    flat = values.astype(jnp.float32)
    row_mean = jnp.mean(flat, axis=-1, keepdims=True)
    centered = flat - row_mean
    row_var = jnp.mean(centered * centered, axis=-1, keepdims=True)
    return (centered * lax.rsqrt(row_var + 1e-5)).astype(jnp.bfloat16)


def add_residual(current, update):
    return (current.astype(jnp.float32) + update).astype(jnp.bfloat16)


def pair_bias(pair_ln, w_bias, form):
    return jnp.einsum(form, pair_ln, w_bias, preferred_element_type=jnp.float32).astype(jnp.bfloat16)


def gated_attention(x_ln, w_in, w_out, bias_hqk, key_mask, batch_first):
    head_dim = w_in.shape[3]
    projected = jnp.einsum('abc,cfhd->abfhd', x_ln, w_in, preferred_element_type=jnp.float32).astype(jnp.bfloat16)
    query = projected[:, :, 0]
    keys = projected[:, :, 1]
    values = projected[:, :, 2]
    gate_raw = projected[:, :, 3]
    if batch_first:
        logits = jnp.einsum('bqhd,bkhd->bhqk', query, keys, preferred_element_type=jnp.float32)
    else:
        logits = jnp.einsum('qbhd,kbhd->bhqk', query, keys, preferred_element_type=jnp.float32)
    logits = logits * head_dim ** -0.5
    if bias_hqk is not None:
        logits = logits + bias_hqk.astype(jnp.float32)
    logits = jnp.where(key_mask > 0, logits, -1e9)
    attn_probs = jax.nn.softmax(logits, axis=-1).astype(jnp.bfloat16)
    if batch_first:
        attended = jnp.einsum('bhqk,bkhd->bqhd', attn_probs, values, preferred_element_type=jnp.float32)
    else:
        attended = jnp.einsum('bhqk,kbhd->qbhd', attn_probs, values, preferred_element_type=jnp.float32)
    gated = (attended * jax.nn.sigmoid(gate_raw.astype(jnp.float32))).astype(jnp.bfloat16)
    return jnp.einsum('abhd,hdc->abc', gated, w_out, preferred_element_type=jnp.float32)


def opm_halves(value_a8, mask_cols, w_in):
    projected = jnp.einsum('sic,cfp->sifp', layer_norm(value_a8), w_in, preferred_element_type=jnp.float32)
    projected = (projected * mask_cols.astype(jnp.float32)[:, :, None, None]).astype(jnp.bfloat16)
    return projected[:, :, 0], projected[:, :, 1]


def opm_update(pair_act, left, right, left_mask, right_mask, w_out):
    outer = jnp.einsum('sip,sjq->ijpq', left, right, preferred_element_type=jnp.float32).astype(jnp.bfloat16)
    update = jnp.einsum('ijpq,pqc->ijc', outer, w_out, preferred_element_type=jnp.float32)
    pair_norm = jnp.einsum('si,sj->ij', left_mask.astype(jnp.bfloat16), right_mask.astype(jnp.bfloat16), preferred_element_type=jnp.float32)
    return add_residual(pair_act, update / (1e-3 + pair_norm)[:, :, None])


def solution(mesh):
    def local_step(value_a7, pair_blk, array_b8, res_mask, w_row_bias, w_row_in, w_row_out, w_col_in, w_col_out, w_opm_in, w_opm_out, w_ts_bias, w_ts_in, w_ts_out, w_te_bias, w_te_in, w_te_out):
        dev_index = lax.axis_index('dap')
        seq_loc = value_a7.shape[0]
        res_loc = pair_blk.shape[0]
        mask_seq = lax.dynamic_slice_in_dim(array_b8, dev_index * seq_loc, seq_loc, 0)
        mask_cols = lax.dynamic_slice_in_dim(array_b8, dev_index * res_loc, res_loc, 1)
        row_keys = mask_seq[:, None, None, :]
        col_keys = mask_cols.T[:, None, None, :]
        tri_keys = res_mask[None, None, None, :]

        row_bias = lax.all_gather(pair_bias(layer_norm(pair_blk), w_row_bias[0], 'ijc,ch->hij'), 'dap', axis=1, tiled=True)
        value_a7 = add_residual(value_a7, gated_attention(layer_norm(value_a7), w_row_in[0], w_row_out[0], row_bias, row_keys, True))
        value_a7 = lax.all_to_all(value_a7, 'dap', 1, 0, tiled=True)
        value_a7 = add_residual(value_a7, gated_attention(layer_norm(value_a7), w_col_in[0], w_col_out[0], None, col_keys, False))
        left, right = opm_halves(value_a7, mask_cols, w_opm_in[0])
        right_full = lax.all_gather(right, 'dap', axis=1, tiled=True)
        pair_blk = opm_update(pair_blk, left, right_full, mask_cols, array_b8, w_opm_out[0])
        pair_ln = layer_norm(pair_blk)
        tri_bias = lax.all_gather(pair_bias(pair_ln, w_ts_bias[0], 'ijc,ch->hij'), 'dap', axis=1, tiled=True)
        pair_blk = add_residual(pair_blk, gated_attention(pair_ln, w_ts_in[0], w_ts_out[0], tri_bias, tri_keys, True))
        pair_blk = lax.all_to_all(pair_blk, 'dap', 1, 0, tiled=True)
        pair_ln = layer_norm(pair_blk)
        tri_bias = lax.all_gather(pair_bias(pair_ln, w_te_bias[0], 'kic,ch->hik'), 'dap', axis=1, tiled=True)
        pair_blk = add_residual(pair_blk, gated_attention(pair_ln, w_te_in[0], w_te_out[0], tri_bias, tri_keys, False))

        row_bias = lax.all_gather(pair_bias(layer_norm(pair_blk), w_row_bias[1], 'ijc,ch->hij'), 'dap', axis=2, tiled=True)
        value_a7 = add_residual(value_a7, gated_attention(layer_norm(value_a7), w_col_in[1], w_col_out[1], None, col_keys, False))
        left, right = opm_halves(value_a7, mask_cols, w_opm_in[1])
        left_full = lax.all_gather(left, 'dap', axis=1, tiled=True)
        pair_blk = opm_update(pair_blk, left_full, right, array_b8, mask_cols, w_opm_out[1])
        value_a7 = lax.all_to_all(value_a7, 'dap', 0, 1, tiled=True)
        value_a7 = add_residual(value_a7, gated_attention(layer_norm(value_a7), w_row_in[1], w_row_out[1], row_bias, row_keys, True))
        pair_ln = layer_norm(pair_blk)
        tri_bias = lax.all_gather(pair_bias(pair_ln, w_te_bias[1], 'kic,ch->hik'), 'dap', axis=1, tiled=True)
        pair_blk = add_residual(pair_blk, gated_attention(pair_ln, w_te_in[1], w_te_out[1], tri_bias, tri_keys, False))
        pair_blk = lax.all_to_all(pair_blk, 'dap', 0, 1, tiled=True)
        pair_ln = layer_norm(pair_blk)
        tri_bias = lax.all_gather(pair_bias(pair_ln, w_ts_bias[1], 'ijc,ch->hij'), 'dap', axis=1, tiled=True)
        pair_blk = add_residual(pair_blk, gated_attention(pair_ln, w_ts_in[1], w_ts_out[1], tri_bias, tri_keys, True))
        return value_a7, pair_blk

    in_specs = (P(('data', 'dap')), P(('data', 'dap')), P('data'), P('data')) + (P(),) * 13
    out_specs = (P(('data', 'dap')), P(('data', 'dap')))
    return jax.shard_map(local_step, mesh=mesh, in_specs=in_specs, out_specs=out_specs, check_vma=False)
```

profile of v0, /device:TPU:96, one launch (start us, length us, event | category | flops | bytes accessed | tf_op | source)
XLA Modules:
  0.0 439.5 jit_solution(8229658000355060932)
XLA Ops:
  18.3 37.1 %all_gather.24 = bf16[12,128,128]{2,0,1:T(8,128)(2,1)S(1)} all-gather(bf16[12,4,128]{2,0,1:T(8,128)(2,1)S(1)} %fusion.104), channel_id=1, replica_groups=mesh['data'=1,'dap'=32] {'dap'}, dimensions={1}, use_global_device_ids=true | all-gather | bytes 405504 | tf_op jit(solution)/shard_map/all_gather | solution.py:71
  55.9 9.5 %fusion.276 = (f32[8,12,128]{2,1,0:T(8,128)S(1)}, f32[8,12,128,128]{2,3,1,0:T(8,128)}) fusion(f32[8,12,128,128]{2,3,1,0:T(8,128)} %fusion.149, f32[12,128,128]{1,2,0:T(8,128)S(1)} %copy.125, pred[8,128]{1,0:T(8,128)(4,1)S(1)} %dynamic-slice_compare_fusion), kind=kOutput, calls=%fused_computation.402 | output fusion | flops 12583039 | bytes 13419520 | tf_op jit(solution)/shard_map/sub | solution.py:38
  65.4 4.7 %fusion.49 = bf16[8,128,384]{2,1,0:T(8,128)(2,1)S(1)} fusion(bf16[8,128,384]{2,1,0:T(8,128)(2,1)S(1)} %copy-done.1, f32[8,12,128,128]{2,3,1,0:T(8,128)} %get-tuple-element.13, f32[8,12,128]{2,1,0:T(8,128)S(1)} %get-tuple-element.12, bf16[8,128,4,12,32]{1,4,3,2,0:T(8,128)(2,1)} %copy-done.10, bf16[2,12,32,384]{3,2,1,0:T(8,128)(2,1)S(1)} %copy-done.30), kind=kOutput, calls=%fused_computation.90 | convolution fusion | flops 409337856 | bytes 9797632 | tf_op jit(solution)/shard_map/abhd,hdc->abc/dot_general | solution.py:44
  81.1 7.6 %all-to-all-done = bf16[8,128,384]{2,0,1:T(8,128)(2,1)S(1)} async-done(((bf16[8,128,384]{2,0,1:T(8,128)(2,1)}), bf16[8,128,384]{2,0,1:T(8,128)(2,1)S(1)}, u32[]{:S(2)}, u32[]{:S(2)}) %all-to-all-start) | async-done | bytes 786464 | tf_op jit(solution)/shard_map/all_to_all | solution.py:73
  94.2 10.8 %fusion.277 = (f32[4,12,256]{2,1,0:T(8,128)S(1)}, f32[4,12,256,256]{2,3,1,0:T(8,128)}) fusion(pred[4,256]{1,0:T(4,128)(4,1)S(1)} %compare_bitcast_fusion, bf16[256,4,4,12,32]{0,4,3,2,1:T(8,128)(2,1)} %convolution_convert_fusion.2), kind=kOutput, calls=%fused_computation.403 | convolution fusion | flops 213909760 | bytes 14205952 | tf_op jit(solution)/shard_map/sub | solution.py:38
  105.0 7.7 %convert_reduce_fusion = (f32[256,4]{0,1:T(4,128)S(1)}, bf16[256,4,384]{2,0,1:T(8,128)(2,1)}) fusion(bf16[2,12,32,384]{3,2,1,0:T(8,128)(2,1)S(1)} %copy-done.29, f32[4,12,256,256]{2,3,1,0:T(8,128)} %get-tuple-element.15, f32[4,12,256]{2,1,0:T(8,128)S(1)} %get-tuple-element.14, bf16[256,4,4,12,32]{0,4,3,2,1:T(8,128)(2,1)} %convolution_convert_fusion.2, ...), kind=kOutput, calls=%fused_computation.45 | convolution fusion | flops 513932288 | bytes 16093184 | tf_op jit(solution)/shard_map/abhd,hdc->abc/dot_general | solution.py:44
  118.9 5.0 %convolution_convert_fusion.1 = bf16[256,4,4,12,32]{0,4,3,2,1:T(8,128)(2,1)} fusion(bf16[2,384,4,12,32]{1,4,3,2,0:T(8,128)(2,1)S(1)} %copy-done.28, bf16[256,4,384]{2,0,1:T(8,128)(2,1)} %get-tuple-element.17, f32[256,4]{0,1:T(4,128)S(1)} %add_rsqrt_fusion.5, f32[256,4]{0,1:T(4,128)S(1)} %broadcast_multiply_fusion.5), kind=kOutput, calls=%fused_computation.50 | convolution fusion | flops 1211105280 | bytes 5120000 | tf_op jit(solution)/shard_map/abc,cfhd->abfhd/dot_general | solution.py:25
  123.9 10.8 %fusion.278 = (f32[4,12,256]{2,1,0:T(8,128)S(1)}, f32[4,12,256,256]{2,3,1,0:T(8,128)}) fusion(pred[4,256]{1,0:T(4,128)(4,1)S(1)} %compare_bitcast_fusion, bf16[256,4,4,12,32]{0,4,3,2,1:T(8,128)(2,1)} %convolution_convert_fusion.1), kind=kOutput, calls=%fused_computation.404 | convolution fusion | flops 213909760 | bytes 14205952 | tf_op jit(solution)/shard_map/sub | solution.py:38
  134.7 7.0 %convert_reduce_fusion.2 = (f32[256,4]{0,1:T(4,128)S(1)}, bf16[256,4,384]{2,0,1:T(8,128)(2,1)S(1)}) fusion(bf16[2,12,32,384]{3,2,1,0:T(8,128)(2,1)} %param.25, f32[4,12,256,256]{2,3,1,0:T(8,128)} %get-tuple-element.19, f32[4,12,256]{2,1,0:T(8,128)S(1)} %get-tuple-element.18, bf16[256,4,4,12,32]{0,4,3,2,1:T(8,128)(2,1)} %convolution_convert_fusion.1, ...), kind=kOutput, calls=%fused_computation.69 | convolution fusion | flops 513932288 | bytes 16076800 | tf_op jit(solution)/shard_map/abhd,hdc->abc/dot_general | solution.py:44
  143.2 4.2 all-to-all-start.1
  149.7 12.1 %all-to-all-done.1 = bf16[256,4,384]{2,1,0:T(4,128)(2,1)S(1)} async-done(((bf16[256,4,384]{2,1,0:T(4,128)(2,1)}), bf16[256,4,384]{2,1,0:T(4,128)(2,1)S(1)}, u32[]{:S(2)}, u32[]{:S(2)}) %all-to-all-start.1) | async-done | bytes 786464 | tf_op jit(solution)/shard_map/all_to_all | solution.py:91
  167.4 4.5 %convolution_convert_fusion = bf16[8,128,4,12,32]{1,4,3,2,0:T(8,128)(2,1)} fusion(bf16[2,384,4,12,32]{1,4,3,2,0:T(8,128)(2,1)} %param.22, bf16[8,128,384,1,1]{2,1,0,3,4:T(8,128)(2,1)S(1)} %copy-done.9), kind=kOutput, calls=%fused_computation.49 | convolution fusion | flops 1209532416 | bytes 5111808 | tf_op jit(solution)/shard_map/abc,cfhd->abfhd/dot_general | solution.py:25
  171.9 4.8 %convert_bitcast_fusion = bf16[4,128,32,32]{2,3,0,1:T(8,128)(2,1)} fusion(bf16[256,128,1,32]{0,3,2,1:T(8,128)(2,1)} %all-gather.5.cloned.1.call-done, bf16[256,4,2,32]{0,3,2,1:T(8,128)(2,1)S(1)} %copy-done.17), kind=kOutput, calls=%fused_computation.30 | convolution fusion | flops 268959744 | bytes 3211264 | tf_op jit(solution)/shard_map/sip,sjq->ijpq/dot_general | solution.py:54
  176.7 6.9 %copy.134 = bf16[4,128,32,32]{1,3,2,0:T(8,128)(2,1)S(1)} copy(bf16[4,128,32,32]{2,3,0,1:T(8,128)(2,1)} %convert_bitcast_fusion) | data formatting | bytes 2097152 | tf_op jit(solution)/shard_map/convert_element_type | solution.py:54
  185.6 33.2 %all_gather.26 = bf16[8,128,128]{2,0,1:T(8,128)(2,1)S(1)} all-gather(bf16[8,4,128]{2,0,1:T(8,128)(2,1)S(1)} %fusion.108), channel_id=1, replica_groups=mesh['data'=1,'dap'=32] {'dap'}, dimensions={1}, use_global_device_ids=true | all-gather | bytes 270336 | tf_op jit(solution)/shard_map/all_gather | solution.py:79
  227.8 4.4 all-to-all-start.2
  232.2 5.1 %fusion.145 = f32[8,12,128,128]{2,3,1,0:T(8,128)} fusion(bf16[8,128,4,12,32]{1,4,3,2,0:T(8,128)(2,1)} %convolution_convert_fusion), kind=kOutput, calls=%fused_computation.203 | convolution fusion | flops 100663296 | bytes 7864320 | tf_op jit(solution)/shard_map/bqhd,bkhd->bhqk/dot_general | solution.py:31
  237.3 4.6 %copy.153 = bf16[256,128,1,32]{1,0,3,2:T(8,128)(2,1)} copy(bf16[256,128,1,32]{0,3,2,1:T(8,128)(2,1)} %all-gather.7.cloned.1.call-done) | data formatting | bytes 4194304 | tf_op jit(solution)/shard_map/all_gather | solution.py:89
  243.4 35.5 %all_gather.27 = bf16[8,128,128]{2,0,1:T(8,128)(2,1)S(1)} all-gather(bf16[8,4,128]{2,0,1:T(8,128)(2,1)S(1)} %fusion.106), channel_id=1, replica_groups=mesh['data'=1,'dap'=32] {'dap'}, dimensions={1}, use_global_device_ids=true | all-gather | bytes 270336 | tf_op jit(solution)/shard_map/all_gather | solution.py:83
  292.6 33.3 %all_gather.30 = bf16[8,128,128]{2,0,1:T(8,128)(2,1)S(1)} all-gather(bf16[8,4,128]{2,0,1:T(8,128)(2,1)S(1)} %fusion.109), channel_id=1, replica_groups=mesh['data'=1,'dap'=32] {'dap'}, dimensions={1}, use_global_device_ids=true | all-gather | bytes 270336 | tf_op jit(solution)/shard_map/all_gather | solution.py:94
  335.8 35.6 %all_gather.28 = bf16[12,128,128]{1,0,2:T(8,128)(2,1)S(1)} all-gather(bf16[12,128,4]{1,0,2:T(8,128)(2,1)S(1)} %fusion.105), channel_id=1, replica_groups=mesh['data'=1,'dap'=32] {'dap'}, dimensions={2}, use_global_device_ids=true | all-gather | bytes 405504 | tf_op jit(solution)/shard_map/all_gather | solution.py:86
  372.1 9.5 %fusion.283 = (f32[8,12,128]{2,1,0:T(8,128)S(1)}, f32[8,12,128,128]{2,3,1,0:T(8,128)}) fusion(f32[8,12,128,128]{2,3,1,0:T(8,128)} %fusion.145, f32[12,128,128]{1,2,0:T(8,128)S(1)} %copy.151, pred[8,128]{1,0:T(8,128)(4,1)S(1)} %copy-done.26), kind=kOutput, calls=%fused_computation.409 | output fusion | flops 12583039 | bytes 13419520 | tf_op jit(solution)/shard_map/sub | solution.py:38
  381.6 5.6 %fusion.52 = bf16[8,128,384]{2,1,0:T(8,128)(2,1)} fusion(f32[8,128,384]{2,1,0:T(8,128)S(1)} %copy-done.4, f32[8,12,128,128]{2,3,1,0:T(8,128)} %get-tuple-element.29, f32[8,12,128]{2,1,0:T(8,128)S(1)} %get-tuple-element.28, bf16[8,128,4,12,32]{1,4,3,2,0:T(8,128)(2,1)} %convolution_convert_fusion, bf16[2,12,32,384]{3,2,1,0:T(8,128)(2,1)S(1)} %copy-done.31), kind=kOutput, calls=%fused_computation.95 | convolution fusion | flops 408944640 | bytes 10584064 | tf_op jit(solution)/shard_map/abhd,hdc->abc/dot_general | solution.py:44
  388.9 33.4 %all_gather.31 = bf16[8,128,128]{2,0,1:T(8,128)(2,1)S(1)} all-gather(bf16[8,4,128]{2,0,1:T(8,128)(2,1)S(1)} %fusion.107), channel_id=1, replica_groups=mesh['data'=1,'dap'=32] {'dap'}, dimensions={1}, use_global_device_ids=true | all-gather | bytes 270336 | tf_op jit(solution)/shard_map/all_gather | solution.py:98
  (190 shorter events, 91.0 us)
Async XLA Ops:
  18.0 37.8 %copy-start.11 = (s32[256,128]{1,0:T(8,128)S(1)}, s32[256,128]{1,0:T(8,128)}, u32[]{:S(2)}) copy-start(s32[256,128]{1,0:T(8,128)} %param.19) | copy-start | bytes 393220
  55.8 9.6 %copy-start.25 = (pred[8,128]{1,0:T(8,128)(4,1)}, pred[8,128]{1,0:T(8,128)(4,1)S(1)}, u32[]{:S(2)}) copy-start(pred[8,128]{1,0:T(8,128)(4,1)S(1)} %dynamic-slice_compare_fusion) | copy-start | bytes 3076
  55.9 9.6 %copy-start.1 = (bf16[8,128,384]{2,1,0:T(8,128)(2,1)S(1)}, bf16[8,128,384]{2,1,0:T(8,128)(2,1)}, u32[]{:S(2)}) copy-start(bf16[8,128,384]{2,1,0:T(8,128)(2,1)} %param.17) | copy-start | bytes 2359300
  55.9 9.6 %copy-start.30 = (bf16[2,12,32,384]{3,2,1,0:T(8,128)(2,1)S(1)}, bf16[2,12,32,384]{3,2,1,0:T(8,128)(2,1)}, u32[]{:S(2)}) copy-start(bf16[2,12,32,384]{3,2,1,0:T(8,128)(2,1)} %param.23) | copy-start | bytes 1769476
  70.2 7.5 %copy-start.33 = (s32[128]{0:T(128)S(1)}, s32[128]{0:T(128)}, u32[]{:S(2)}) copy-start(s32[128]{0:T(128)} %param.20) | copy-start | bytes 1540
  71.5 8.1 %copy-start.2 = (bf16[2,288,4,8,36]{1,3,4,2,0:T(8,128)(2,1)S(1)}, bf16[2,288,4,8,36]{1,3,4,2,0:T(8,128)(2,1)}, u32[]{:S(2)}) copy-start(bf16[2,288,4,8,36]{1,3,4,2,0:T(8,128)(2,1)} %param.29) | copy-start | bytes 3981316
  71.5 17.1 %all-to-all-start = ((bf16[8,128,384]{2,0,1:T(8,128)(2,1)}), bf16[8,128,384]{2,0,1:T(8,128)(2,1)S(1)}, u32[]{:S(2)}, u32[]{:S(2)}) async-start(bf16[8,128,384]{2,0,1:T(8,128)(2,1)} %copy.127), calls=%async_computation | async-start | bytes 1572864 | tf_op jit(solution)/shard_map/all_to_all | solution.py:73
  75.3 96.6 %all-gather.5.cloned.1.call-start = ((), (), s32[]{:S(2)}) async-start(), calls=%async_computation.4 | async-start | bytes 2162688 | tf_op jit(solution)/shard_map/all_gather | solution.py:76
  77.6 143.3 %copy-start.34 = (pred[128]{0:T(512)(128)(4,1)}, pred[128]{0:T(512)(128)(4,1)S(1)}, u32[]{:S(2)}) copy-start(pred[128]{0:T(512)(128)(4,1)S(1)} %broadcast_compare_fusion) | copy-start | bytes 388
  94.2 10.8 %copy-start.29 = (bf16[2,12,32,384]{3,2,1,0:T(8,128)(2,1)S(1)}, bf16[2,12,32,384]{3,2,1,0:T(8,128)(2,1)}, u32[]{:S(2)}) copy-start(bf16[2,12,32,384]{3,2,1,0:T(8,128)(2,1)} %param.25) | copy-start | bytes 1769476
  105.0 9.4 %copy-start.32 = (bf16[2,384,2,32]{1,3,2,0:T(8,128)(2,1)S(1)}, bf16[2,384,2,32]{1,3,2,0:T(8,128)(2,1)}, u32[]{:S(2)}) copy-start(bf16[2,384,2,32]{1,3,2,0:T(8,128)(2,1)} %param.26) | copy-start | bytes 294916
  116.1 7.7 %copy-start.16 = (bf16[256,4,2,32]{0,3,2,1:T(8,128)(2,1)}, bf16[256,4,2,32]{0,3,2,1:T(8,128)(2,1)S(1)}, u32[]{:S(2)}) copy-start(bf16[256,4,2,32]{0,3,2,1:T(8,128)(2,1)S(1)} %fusion.98) | copy-start | bytes 393220
  123.9 10.8 %copy-start.8 = (bf16[256,4,384]{2,0,1:T(8,128)(2,1)S(1)}, bf16[256,4,384]{2,0,1:T(8,128)(2,1)}, u32[]{:S(2)}) copy-start(bf16[256,4,384]{2,0,1:T(8,128)(2,1)} %get-tuple-element.17) | copy-start | bytes 2359300
  143.2 18.6 %all-to-all-start.1 = ((bf16[256,4,384]{2,1,0:T(4,128)(2,1)}), bf16[256,4,384]{2,1,0:T(4,128)(2,1)S(1)}, u32[]{:S(2)}, u32[]{:S(2)}) async-start(bf16[256,4,384]{2,1,0:T(4,128)(2,1)} %copy.132), calls=%async_computation.1 | async-start | bytes 1572864 | tf_op jit(solution)/shard_map/all_to_all | solution.py:91
  147.4 89.9 %all-gather.7.cloned.1.call-start = ((), (), s32[]{:S(2)}) async-start(), calls=%async_computation.5 | async-start | bytes 2162688 | tf_op jit(solution)/shard_map/all_gather | solution.py:89
  148.9 13.7 %copy-start.20 = (bf16[256,4,2,32]{0,3,2,1:T(8,128)(2,1)}, bf16[256,4,2,32]{0,3,2,1:T(8,128)(2,1)S(1)}, u32[]{:S(2)}) copy-start(bf16[256,4,2,32]{0,3,2,1:T(8,128)(2,1)S(1)} %fusion.99) | copy-start | bytes 393220
  185.3 33.7 %copy-start = (bf16[1,288,4,8,36]{1,3,4,2,0:T(8,128)(2,1)S(1)}, bf16[1,288,4,8,36]{1,3,4,2,0:T(8,128)(2,1)}, u32[]{:S(2)}) copy-start(bf16[1,288,4,8,36]{1,3,4,2,0:T(8,128)(2,1)} %get-tuple-element.3) | copy-start | bytes 1990660
  227.8 14.0 %all-to-all-start.2 = ((bf16[4,128,288]{2,0,1:T(4,128)(2,1)}), bf16[4,128,288]{2,0,1:T(4,128)(2,1)S(1)}, u32[]{:S(2)}, u32[]{:S(2)}) async-start(bf16[4,128,288]{2,0,1:T(4,128)(2,1)} %copy.139), calls=%async_computation.2 | async-start | bytes 786432 | tf_op jit(solution)/shard_map/all_to_all | solution.py:81
  291.8 34.4 %copy-start.36 = (pred[128]{0:T(512)(128)(4,1)S(1)}, pred[128]{0:T(512)(128)(4,1)}, u32[]{:S(2)}) copy-start(pred[128]{0:T(512)(128)(4,1)} %copy-done.34) | copy-start | bytes 388
  328.5 7.2 %copy-start.19 = (bf16[1,288,12]{1,0,2:T(2,128)(2,1)S(1)}, bf16[1,288,12]{1,0,2:T(2,128)(2,1)}, u32[]{:S(2)}) copy-start(bf16[1,288,12]{1,0,2:T(2,128)(2,1)} %get-tuple-element.10) | copy-start | bytes 20740
  331.8 55.5 %all-to-all-start.3 = ((bf16[128,4,288]{2,1,0:T(4,128)(2,1)}), bf16[128,4,288]{2,1,0:T(4,128)(2,1)S(1)}, u32[]{:S(2)}, u32[]{:S(2)}) async-start(bf16[128,4,288]{2,1,0:T(4,128)(2,1)} %copy.158), calls=%async_computation.3 | async-start | bytes 786432 | tf_op jit(solution)/shard_map/all_to_all | solution.py:96
  335.5 36.5 %copy-start.26 = (pred[8,128]{1,0:T(8,128)(4,1)S(1)}, pred[8,128]{1,0:T(8,128)(4,1)}, u32[]{:S(2)}) copy-start(pred[8,128]{1,0:T(8,128)(4,1)} %copy-done.25) | copy-start | bytes 3076
  372.1 9.6 %copy-start.4 = (f32[8,128,384]{2,1,0:T(8,128)S(1)}, f32[8,128,384]{2,1,0:T(8,128)}, u32[]{:S(2)}) copy-start(f32[8,128,384]{2,1,0:T(8,128)} %reshape.300) | copy-start | bytes 4718596
  372.1 9.6 %copy-start.31 = (bf16[2,12,32,384]{3,2,1,0:T(8,128)(2,1)S(1)}, bf16[2,12,32,384]{3,2,1,0:T(8,128)(2,1)}, u32[]{:S(2)}) copy-start(bf16[2,12,32,384]{3,2,1,0:T(8,128)(2,1)} %param.23) | copy-start | bytes 1769476
  (19 other events, 50.5 us)
Sparse Core Ops, SparseCore 0:
  117.0 39.2 all-gather.4
  158.3 39.7 all-gather.6
where the time goes:
time: 448 us; the launch traced here: 440 us
  blocking collectives  208 us (46%)
  matrix products  114 us (25%)
  local copies, waits for them, and re-layouts  34.2 us (8%)
  other arithmetic  30.8 us (7%)
  waiting for transfers between devices  19.8 us (4%)
  starting transfers between devices  16.8 us (4%)
  between operations  15.4 us (3%)
    all_gather x1, blocking collectives, local_step(): lax.all_gather(pair_bias(layer_norm(pair_blk), w_row_bias[0], 'ijc,ch->hi...  37.1 us
    all_gather x1, blocking collectives, local_step(): lax.all_gather(pair_bias(layer_norm(pair_blk), w_row_bias[1], 'ijc,ch->hi...  35.6 us
    all_gather x1, blocking collectives, local_step(): lax.all_gather(pair_bias(pair_ln, w_te_bias[0], 'kic,ch->hik'), 'dap', ax...  35.5 us
    dot_general x8, matrix products, gated_attention(): jnp.einsum('abhd,hdc->abc', gated, w_out, preferred_element_type=jnp.floa...  35.4 us
    sub x6, matrix products, gated_attention(): attn_probs = jax.nn.softmax(logits, axis=-1).astype(jnp.bfloat16)  34.2 us
    all_gather x1, blocking collectives, local_step(): lax.all_gather(pair_bias(pair_ln, w_ts_bias[1], 'ijc,ch->hij'), 'dap', ax...  33.4 us
    all_gather x1, blocking collectives, local_step(): lax.all_gather(pair_bias(pair_ln, w_te_bias[1], 'kic,ch->hik'), 'dap', ax...  33.3 us
    all_gather x1, blocking collectives, local_step(): lax.all_gather(pair_bias(pair_ln, w_ts_bias[0], 'ijc,ch->hij'), 'dap', ax...  33.2 us
  transfers between devices with their start and end apart: 6, of which 2 were waited for; matrix products, arithmetic and copies ran while one was open for 21% of the time, Pallas kernels for 0%

commit v1 on v0

v1 whole, which is shorter than its diff:
```python
import functools

import jax
import jax.numpy as jnp
from jax import lax
from jax.experimental import pallas as pl
from jax.experimental.pallas import tpu as pltpu
from jax.sharding import PartitionSpec as P

F32 = jnp.float32
BF16 = jnp.bfloat16
EPS = 1e-5
NEG = -1e9
NN = (((1,), (0,)), ((), ()))
NT = (((1,), (1,)), ((), ()))
TN = (((0,), (0,)), ((), ()))
MESH = pl.DeviceIdType.MESH


def mm(a, b, dims=NN):
    return lax.dot_general(a, b, dims, preferred_element_type=F32)


def norm_axis(x, axis):
    mean = jnp.mean(x, axis=axis, keepdims=True)
    centered = x - mean
    var = jnp.mean(centered * centered, axis=axis, keepdims=True)
    return (centered * lax.rsqrt(var + EPS)).astype(BF16)


def one_hot(rows, cols, source):
    r = lax.broadcasted_iota(jnp.int32, (rows, cols), 0)
    c = lax.broadcasted_iota(jnp.int32, (rows, cols), 1)
    return jnp.where(c == source(r), 1.0, 0.0).astype(BF16)


def swap_matrix(a, b):
    return one_hot(a * b, a * b, lambda r: (r % a) * b + r // a)


def softmax_cols(t):
    e = jnp.exp(t - jnp.max(t, axis=0, keepdims=True))
    return (e * (1.0 / jnp.sum(e, axis=0, keepdims=True))).astype(BF16)


EXCHANGES = ('b1', 'm1', 'c', 's1', 'z1', 'e1', 'b2', 'a', 'm2', 'e2', 'z2', 's2')


def step_kernel(cfg, *refs):
    n, sl, rl, S, R, CM, CZ, H, D, HT, DT, OP, HP = cfg
    WM = H * D
    WT = HT * DT
    it = iter(refs)
    (m_ref, z_ref, mask_ref, rmask_ref, wb_hbm, wr_hbm, wro_hbm, wc_hbm, wco_hbm, wpi_hbm, wpo_hbm,
     wsb_hbm, ws_hbm, wso_hbm, web_hbm, we_hbm, weo_hbm) = [next(it) for _ in range(17)]
    m_out, z_out = next(it), next(it)
    wb, wr, wro, wc, wco, wpi, wpo, wsb, ws, wso, web, we, weo = weights = [next(it) for _ in range(13)]
    bias_f, biast_f = next(it), next(it)
    xz, qkvg, pbuf, vbuf = [next(it) for _ in range(4)]
    qvg, kbuf, gbuf = [next(it) for _ in range(3)]
    mrow, mcol, zb, znb = [next(it) for _ in range(4)]
    abuf, cbuf, abuf2, cbuf2, perm, obuf = [next(it) for _ in range(6)]
    mcolmask, seqmask, rmaskt, colmask, norm_ref = [next(it) for _ in range(5)]
    send = {}
    recv = {}
    for name in EXCHANGES:
        send[name] = next(it)
        recv[name] = next(it)
    send_sem, recv_sem, w_sem = next(it), next(it), next(it)
    hbm = [wb_hbm, wr_hbm, wro_hbm, wc_hbm, wco_hbm, wpi_hbm, wpo_hbm, wsb_hbm, ws_hbm, wso_hbm, web_hbm, we_hbm, weo_hbm]
    loads = [pltpu.make_async_copy(src, dst, w_sem.at[i]) for i, (src, dst) in enumerate(zip(hbm, weights))]
    for load in loads:
        load.start()
    (ld_wb, ld_wr, ld_wro, ld_wc, ld_wco, ld_wpi, ld_wpo, ld_wsb, ld_ws, ld_wso, ld_web, ld_we, ld_weo) = loads

    me = lax.axis_index('dap')
    barrier = pltpu.get_barrier_semaphore()

    @pl.loop(1, n)
    def _(k):
        pl.semaphore_signal(barrier, inc=1, device_id={'dap': lax.rem(me + k, n)}, device_id_type=MESH)

    def push(name, scatter):
        x = EXCHANGES.index(name)
        src, dst = send[name], recv[name]

        @pl.loop(1, n)
        def _(k):
            peer = lax.rem(me + k, n)
            pltpu.make_async_remote_copy(
                src_ref=src.at[peer] if scatter else src, dst_ref=dst.at[me], send_sem=send_sem.at[x],
                recv_sem=recv_sem.at[x], device_id={'dap': peer}, device_id_type=MESH).start()
        dst[me] = src[me] if scatter else src[...]

    def bulk_wait(name, sems):
        x = EXCHANGES.index(name)
        bulk = recv[name].at[pl.ds(0, n - 1)]
        pltpu.make_async_copy(bulk, bulk, sems.at[x]).wait()

    def arrived(name):
        bulk_wait(name, recv_sem)

    eye = one_hot(R, R, lambda r: r)

    def pair_norm(zref):
        for i in range(rl):
            xz[:, i * R:(i + 1) * R] = norm_axis(zref[i].astype(F32), 0)

    def bias_block(name, w, heads):
        got = mm(w, xz[...]).astype(BF16).astype(F32)
        send[name][...] = jnp.concatenate([got[:, i * R:(i + 1) * R] for i in range(rl)], axis=0).astype(BF16)
        push(name, False)

    def bias_build(name, heads, padded, dst, transpose):
        group = R // (rl * padded)
        swap = swap_matrix(group * rl, padded)
        rows = group * rl

        @pl.loop(0, n // group)
        def _(g):
            got = mm(swap, recv[name][pl.ds(g * group, group)].reshape(R, R))
            at = pl.ds(pl.multiple_of(g * rows, rows), rows)
            for h in range(heads):
                dst[h, at, :] = got[h * rows:(h + 1) * rows]
        if transpose:
            @pl.loop(0, heads)
            def _(h):
                dst[h] = dst[h].T

    def pair_project(w):
        got = mm(w, xz[...])
        for i in range(rl):
            qkvg[i] = got[:, i * R:(i + 1) * R].astype(BF16)

    def pair_attend(zref, wo, dst):
        scale = DT ** -0.5
        lane_head = lax.broadcasted_iota(jnp.int32, (R, WT), 1) % HT
        sub_head = lax.broadcasted_iota(jnp.int32, (WT, R), 0) % HT

        @pl.loop(0, rl)
        def _(i):
            qt = qkvg[i, 0:WT]
            k = qkvg[i, WT:2 * WT].astype(F32).T
            vt = qkvg[i, 2 * WT:3 * WT].astype(F32)
            for h in range(HT):
                kh = jnp.where(lane_head == h, k, 0.0).astype(BF16)
                t = mm(kh, qt) * scale + biast_f[h]
                t = jnp.where(rmaskt[...] > 0, t, NEG)
                pbuf[h * R:(h + 1) * R, :] = softmax_cols(t)
                vbuf[:, h * R:(h + 1) * R] = jnp.where(sub_head == h, vt, 0.0).astype(BF16)
            o = mm(vbuf[...], pbuf[...])
            gated = (o * jax.nn.sigmoid(qkvg[i, 3 * WT:4 * WT].astype(F32))).astype(BF16)
            dst[i] = (zref[i].astype(F32) + mm(wo, gated)).astype(BF16)

    def pair_send(name):
        for i in range(rl):
            znb[i] = zb[i].astype(F32).T.astype(BF16)
        swap = one_hot(4 * rl * rl, 4 * rl * rl, lambda r: (r % rl) * (4 * rl) + r // rl)
        width = 4 * rl

        @pl.loop(0, n // 4)
        def _(g):
            got = znb[:, pl.ds(pl.multiple_of(g * width, width), width), :].reshape(rl * width, CZ)
            send[name][pl.ds(g * 4, 4)] = mm(swap, got).astype(BF16).reshape(4, rl * rl, CZ)
        push(name, True)

    def pair_receive(name):
        rows = 8 * rl
        swap = one_hot(rows * rl, rows * rl, lambda r: ((r % rows) // rl) * (rl * rl) + (r // rows) * rl + r % rl)

        @pl.loop(0, n // 8)
        def _(g):
            got = mm(swap, recv[name][pl.ds(g * 8, 8)].reshape(rows * rl, CZ)).astype(BF16)
            at = pl.ds(pl.multiple_of(g * rows, rows), rows)
            for i in range(rl):
                znb[i, at, :] = got[i * rows:(i + 1) * rows]
        for i in range(rl):
            zb[i] = znb[i].astype(F32).T.astype(BF16)

    def outer_update(name, left, wo, zref, dst):
        swap = swap_matrix(4 * rl, 16)
        width = 4 * rl

        @pl.loop(0, n // 4)
        def _(g):
            for half in range(OP // 16):
                got = recv[name][pl.ds(g * 4, 4)].reshape(width, OP, S)[:, half * 16:(half + 1) * 16].reshape(width * 16, S)
                perm[half * 16:(half + 1) * 16, pl.ds(pl.multiple_of(g * width, width), width), :] = mm(swap, got).astype(BF16).reshape(16, width, S)

        @pl.loop(0, OP // 2)
        def _(t):
            o = mm(left[...], perm[pl.ds(t * 2, 2)].reshape(2 * R, S), NT).astype(BF16)
            for u in range(2):
                at = pl.ds(pl.multiple_of((t * 2 + u) * OP, OP), OP)
                for i in range(rl):
                    obuf[at, i * R:(i + 1) * R] = o[i * OP:(i + 1) * OP, u * R:(u + 1) * R]
        upd = mm(wo, obuf[...])
        for i in range(rl):
            dst[i] = (zref[i].astype(F32) + upd[:, i * R:(i + 1) * R] * (1.0 / (1e-3 + norm_ref[i:i + 1, :]))).astype(BF16)

    def project(x, w):
        qvg[0:WM] = mm(w[0:WM], x, NT).astype(BF16)
        kbuf[...] = mm(x, w[WM:2 * WM], NT).astype(BF16)
        qvg[WM:3 * WM] = mm(w[2 * WM:4 * WM], x, NT).astype(BF16)

    per_tile = 128 // D

    def attend(lo, size, mask, bias):
        scale = D ** -0.5
        lane_head = lax.broadcasted_iota(jnp.int32, (size, 128), 1) // D
        at = slice(lo, lo + size)
        for h in range(H):
            tile = (h // per_tile) * 128
            kh = jnp.where(lane_head == h % per_tile, kbuf[at, tile:tile + 128].astype(F32), 0.0).astype(BF16)
            t = mm(kh, qvg[tile:tile + 128, at]) * scale
            if bias is not None:
                t = t + bias[h]
            t = jnp.where(mask > 0, t, NEG)
            o = mm(qvg[WM + h * D:WM + (h + 1) * D, at], softmax_cols(t))
            g = qvg[2 * WM + h * D:2 * WM + (h + 1) * D, at].astype(F32)
            gbuf[h * D:(h + 1) * D, at] = (o * jax.nn.sigmoid(g)).astype(BF16)

    def row_attention(src, w, wo, bias, dst):
        @pl.loop(0, sl // 2)
        def _(t):
            xf = src[pl.ds(2 * t, 2)].astype(F32).reshape(2 * R, CM)
            project(norm_axis(xf, 1), w)
            for u in range(2):
                row = seqmask[pl.ds(2 * t + u, 1), :]
                mask = mm(eye, jnp.broadcast_to(row, (R, R)).astype(BF16), NT)
                attend(u * R, R, mask, bias)
            upd = mm(gbuf[...], wo[...], TN)
            dst[pl.ds(2 * t, 2)] = (xf + upd).astype(BF16).reshape(2, R, CM)

    def col_attention(load, w, wo, wp, a_dst, c_dst):
        @pl.loop(0, rl)
        def _(i):
            xf = load(i)
            project(norm_axis(xf, 1), w)
            pick = jnp.where(lax.broadcasted_iota(jnp.int32, (R, R), 0) == me * rl + i, 1.0, 0.0).astype(BF16)
            mask = mm(mcolmask[...], pick)
            attend(0, S, jnp.concatenate([mask, mask], axis=1), None)
            y = (xf + mm(gbuf[...], wo[...], TN)).astype(BF16)
            mcol[i] = y
            x = norm_axis(y.astype(F32), 1)
            half = (mm(wp, x, NT) * colmask[pl.ds(i, 1), :]).astype(BF16)
            at = pl.ds(pl.multiple_of(i * OP, OP), OP)
            a_dst[at, :] = half[0:OP]
            c_dst[at, :] = half[OP:2 * OP]

    maskf = mask_ref[...].astype(F32).astype(BF16)
    mcolmask[...] = maskf
    seqmask[...] = mask_ref[pl.ds(pl.multiple_of(me * sl, sl), sl), :].astype(F32)
    rmaskt[...] = mm(eye, jnp.broadcast_to(rmask_ref[...].astype(F32), (R, R)).astype(BF16), NT)
    pick = jnp.where(lax.broadcasted_iota(jnp.int32, (8, R), 1) == lax.broadcasted_iota(jnp.int32, (8, R), 0) + me * rl, 1.0, 0.0).astype(BF16)
    colmask[...] = mm(pick, maskf, NT)
    norm_ref[...] = mm(colmask[...].astype(BF16), maskf)

    pair_norm(z_ref)
    ld_wb.wait()
    pl.semaphore_wait(barrier, n - 1)
    bias_block('b1', wb[0], HP)
    ld_wr.wait()
    ld_wro.wait()
    arrived('b1')
    bias_build('b1', H, HP, bias_f, True)
    row_attention(m_ref, wr.at[0], wro.at[0], bias_f, mrow)

    swap = one_hot(16 * sl, 16 * sl, lambda r: (r % sl) * 16 + r // sl)

    @pl.loop(0, R // 16)
    def _(g):
        got = mrow[:, pl.ds(pl.multiple_of(g * 16, 16), 16), :].reshape(sl * 16, CM)
        send['m1'][pl.ds(g * (16 // rl), 16 // rl)] = mm(swap, got).astype(BF16).reshape(16 // rl, rl * sl, CM)
    push('m1', True)
    ld_wc.wait()
    ld_wco.wait()
    ld_wpi.wait()
    arrived('m1')

    def load_first(i):
        got = recv['m1'][:, pl.ds(pl.multiple_of((i // 2) * 16, 16), 16), :].astype(F32)
        return jnp.where(i % 2 == 0, got[:, 0:sl], got[:, sl:2 * sl]).reshape(S, CM)

    col_attention(load_first, wc.at[0], wco.at[0], wpi[0], abuf, send['c'])
    push('c', False)
    col_attention(lambda i: mcol[i].astype(F32), wc.at[1], wco.at[1], wpi[1], send['a'], cbuf2)
    push('a', False)

    for p in range(rl // 2):
        pair = [mcol[2 * p + u].astype(F32).reshape(n, sl, CM) for u in range(2)]
        send['m2'][:, p * 2 * sl:(p + 1) * 2 * sl, :] = jnp.concatenate(pair, axis=1).astype(BF16)
    push('m2', True)

    for load in (ld_wpo, ld_wsb, ld_ws, ld_wso, ld_web, ld_we, ld_weo):
        load.wait()
    arrived('c')
    outer_update('c', abuf, wpo[0], z_ref, zb)
    pair_norm(zb)
    bias_block('s1', wsb[0], HT)
    pair_project(ws[0])
    arrived('s1')
    bias_build('s1', HT, HT, biast_f, True)
    pair_attend(zb, wso[0], zb)
    pair_send('z1')
    pair_norm(zb)
    bias_block('e1', web[0], HT)
    arrived('z1')
    pair_receive('z1')
    pair_norm(zb)
    pair_project(we[0])
    arrived('e1')
    bias_build('e1', HT, HT, biast_f, False)
    pair_attend(zb, weo[0], zb)

    pair_norm(zb)
    bias_block('b2', wb[1], HP)
    arrived('a')
    outer_update('a', cbuf2, wpo[1], zb, zb)
    pair_norm(zb)
    bias_block('e2', web[1], HT)
    pair_project(we[1])

    arrived('m2')
    back = one_hot(16 * sl, 16 * sl, lambda r: (r % 16) * sl + r // 16)

    @pl.loop(0, R // 16)
    def _(g):
        got = recv['m2'][pl.ds(g * (16 // rl), 16 // rl)].reshape(16 * sl, CM)
        mrow[:, pl.ds(pl.multiple_of(g * 16, 16), 16), :] = mm(back, got).astype(BF16).reshape(sl, 16, CM)
    arrived('b2')
    bias_build('b2', H, HP, bias_f, False)
    row_attention(mrow, wr.at[1], wro.at[1], bias_f, m_out)

    arrived('e2')
    bias_build('e2', HT, HT, biast_f, True)
    pair_attend(zb, weo[1], zb)
    pair_send('z2')
    pair_norm(zb)
    bias_block('s2', wsb[1], HT)
    arrived('z2')
    pair_receive('z2')
    pair_norm(zb)
    pair_project(ws[1])
    arrived('s2')
    bias_build('s2', HT, HT, biast_f, False)
    pair_attend(zb, wso[1], z_out)
    for name in EXCHANGES:
        bulk_wait(name, send_sem)


def solution(mesh):
    n = mesh.shape['dap']

    def local_step(m, z, mask, rmask, w_row_bias, w_row_in, w_row_out, w_col_in, w_col_out, w_opm_in, w_opm_out, w_ts_bias, w_ts_in, w_ts_out, w_te_bias, w_te_in, w_te_out):
        sl, R, CM = m.shape
        rl, _, CZ = z.shape
        S = mask.shape[0]
        H, D = w_row_in.shape[3:]
        HT, DT = w_ts_in.shape[3:]
        OP = w_opm_in.shape[3]
        HP = -(-H // 8) * 8
        WM, WT = H * D, HT * DT
        zt = z.transpose(0, 2, 1)
        wb = jnp.pad(w_row_bias.transpose(0, 2, 1), ((0, 0), (0, HP - H), (0, 0)))
        wr = w_row_in.transpose(0, 2, 3, 4, 1).reshape(2, 4 * WM, CM)
        wc = w_col_in.transpose(0, 2, 3, 4, 1).reshape(2, 4 * WM, CM)
        wro = w_row_out.reshape(2, WM, CM)
        wco = w_col_out.reshape(2, WM, CM)
        wpi = w_opm_in.transpose(0, 2, 3, 1).reshape(2, 2 * OP, CM)
        wpo = jnp.stack([w_opm_out[0].transpose(2, 1, 0).reshape(CZ, OP * OP), w_opm_out[1].transpose(2, 0, 1).reshape(CZ, OP * OP)])
        wsb = w_ts_bias.transpose(0, 2, 1)
        web = w_te_bias.transpose(0, 2, 1)
        ws = w_ts_in.transpose(0, 2, 4, 3, 1).reshape(2, 4 * WT, CZ)
        we = w_te_in.transpose(0, 2, 4, 3, 1).reshape(2, 4 * WT, CZ)
        wso = w_ts_out.transpose(0, 3, 2, 1).reshape(2, CZ, WT)
        weo = w_te_out.transpose(0, 3, 2, 1).reshape(2, CZ, WT)
        weights = [wb, wr, wro, wc, wco, wpi, wpo, wsb, ws, wso, web, we, weo]

        def vm(shape, dtype=BF16):
            return pltpu.VMEM(shape, dtype)
        scratch = [vm(w.shape) for w in weights]
        scratch += [vm((H, R, R), F32), vm((HT, R, R), F32)]
        scratch += [vm((CZ, rl * R)), vm((rl, 4 * WT, R)), vm((HT * R, R)), vm((WT, HT * R))]
        scratch += [vm((3 * WM, S)), vm((S, WM)), vm((WM, S))]
        scratch += [vm((sl, R, CM)), vm((rl, S, CM)), vm((rl, CZ, R)), vm((rl, R, CZ))]
        scratch += [vm((rl * OP, S))] * 4 + [vm((OP, R, S)), vm((OP * OP, rl * R))]
        scratch += [vm((S, R)), vm((sl, R), F32), vm((R, R), F32), vm((8, S), F32), vm((8, R), F32)]
        bias_row, bias_tri = (rl * HP, R), (rl * HT, R)
        shapes = {'b1': bias_row, 'b2': bias_row, 's1': bias_tri, 'e1': bias_tri, 'e2': bias_tri, 's2': bias_tri,
                  'c': (rl * OP, S), 'a': (rl * OP, S), 'm1': (rl * sl, CM), 'm2': (rl * sl, CM), 'z1': (rl * rl, CZ), 'z2': (rl * rl, CZ)}
        for name in EXCHANGES:
            shape = shapes[name]
            scratch += [vm((n,) + shape if name[0] in 'mz' else shape), vm((n,) + shape)]
        scratch += [pltpu.SemaphoreType.DMA((len(EXCHANGES),)), pltpu.SemaphoreType.DMA((len(EXCHANGES),)), pltpu.SemaphoreType.DMA((len(weights),))]
        cfg = (n, sl, rl, S, R, CM, CZ, H, D, HT, DT, OP, HP)
        vmem = pl.BlockSpec(memory_space=pltpu.VMEM)
        hbm = pl.BlockSpec(memory_space=pl.ANY)
        m_new, z_new = pl.pallas_call(
            functools.partial(step_kernel, cfg),
            out_shape=[jax.ShapeDtypeStruct(m.shape, BF16), jax.ShapeDtypeStruct(zt.shape, BF16)],
            in_specs=[vmem] * 4 + [hbm] * len(weights),
            out_specs=[vmem, vmem],
            scratch_shapes=scratch,
            compiler_params=pltpu.CompilerParams(collective_id=0, has_side_effects=True, vmem_limit_bytes=60 * 2**20),
            name='evoformer',
        )(m, zt, mask, rmask.reshape(1, R), *weights)
        return m_new, z_new.transpose(0, 2, 1)

    in_specs = (P(('data', 'dap')), P(('data', 'dap')), P('data'), P('data')) + (P(),) * 13
    out_specs = (P(('data', 'dap')), P(('data', 'dap')))
    return jax.shard_map(local_step, mesh=mesh, in_specs=in_specs, out_specs=out_specs, check_vma=False)
```

time: 448 us -> 237 us (0.53)
  the two profiles are of different devices: /device:TPU:96 before, /device:TPU:97 now
where the time goes in v1:
time: 237 us; the launch traced here: 236 us
  Pallas kernels  227 us (96%)
  local copies, waits for them, and re-layouts  7.8 us (3%)
    pallas_call x1, Pallas kernels, local_step(): pl.pallas_call(functools.partial(step_kernel, cfg), out_shape=[jax.ShapeD...  227 us

profile of v1, /device:TPU:97, one launch (start us, length us, event | category | flops | bytes accessed | tf_op | source)
XLA Modules:
  0.0 236.4 jit_solution(8981885824489678314)
XLA Ops:
  0.6 1.5 slice_bitcast_fusion
  2.2 0.3 copy.25
  2.4 0.3 copy.26
  2.7 0.0 copy-start
  2.7 0.3 copy.27
  3.0 0.0 copy-start.1
  3.0 0.0 copy-start.3
  3.0 1.1 pad_maximum_fusion.refs_10_
  4.1 0.0 copy-done
  4.1 1.0 copy.28.refs_13_
  5.1 0.0 copy-done.1
  5.1 1.0 copy.29.refs_16_
  6.1 0.0 copy-done.3
  6.1 0.6 pad.4.refs_4_
  6.7 226.8 %evoformer.1 = (bf16[8,128,384]{2,1,0:T(8,128)(2,1)}, bf16[4,288,128]{2,1,0:T(8,128)(2,1)}) custom-call(bf16[8,128,384]{2,1,0:T(8,128)(2,1)} %refs_0_.1, bf16[4,288,128]{2,1,0:T(8,128)(2,1)} %bitcast.51, s32[256,128]{1,0:T(8,128)} %refs_2_.1, s32[1,128]{1,0:T(1,128)} %bitcast.57, bf16[2,16,288]{2,1,0:T(8,128)(2,1)} %pad.4.refs_4_, ...), custom_call_target="tpu_custom_call" | custom-call | tf_op jit(solution)/shard_map/evoformer/pallas_call | solution.py:399
  233.6 0.0 copy-start.2
  233.6 2.1 copy.34
  235.7 0.0 copy-done.2
  235.7 0.7 copy.35
  (1 shorter events, 0.0 us)
Async XLA Ops:
  2.7 1.4 copy-start
  3.0 2.1 copy-start.1
  3.0 3.1 %copy-start.3 = (bf16[2,288,12]{1,0,2:T(2,128)(2,1)S(1)}, bf16[2,288,12]{1,0,2:T(2,128)(2,1)}, u32[]{:S(2)}) copy-start(bf16[2,288,12]{1,0,2:T(2,128)(2,1)} %param.21) | copy-start | bytes 41476
  233.6 2.1 copy-start.2

commit v2 on v1

v2 whole, which is shorter than its diff:
```python
import functools
import math

import jax
import jax.numpy as jnp
from jax import lax
from jax.experimental import pallas as pl
from jax.experimental.pallas import tpu as pltpu
from jax.sharding import PartitionSpec as P

F32 = jnp.float32
BF16 = jnp.bfloat16
EPS = 1e-5
LOG2E = 1.4426950408889634
NEG = -1e9 * LOG2E
NN = (((1,), (0,)), ((), ()))
NT = (((1,), (1,)), ((), ()))
TN = (((0,), (0,)), ((), ()))
MESH = pl.DeviceIdType.MESH


def mm(a, b, dims=NN):
    return lax.dot_general(a, b, dims, preferred_element_type=F32)


def norm_axis(x, axis):
    mean = jnp.mean(x, axis=axis, keepdims=True)
    centered = x - mean
    var = jnp.mean(centered * centered, axis=axis, keepdims=True)
    return (centered * lax.rsqrt(var + EPS)).astype(BF16)


def one_hot(rows, cols, source):
    r = lax.broadcasted_iota(jnp.int32, (rows, cols), 0)
    c = lax.broadcasted_iota(jnp.int32, (rows, cols), 1)
    return jnp.where(c == source(r), 1.0, 0.0).astype(BF16)


def swap_matrix(a, b):
    return one_hot(a * b, a * b, lambda r: (r % a) * b + r // a)


def softmax_cols(t):
    e = jnp.exp2(t - jnp.max(t, axis=0, keepdims=True))
    return (e * (1.0 / jnp.sum(e, axis=0, keepdims=True))).astype(BF16)


EXCHANGES = ('b1', 'm1', 'c', 's1', 'z1', 'e1', 'b2', 'a', 'm2', 'e2', 'z2', 's2')
FLOWS = ('b1', 'm1_0', 'm1_1', 's1', 'z1', 'e1', 'b2', 'm2_0', 'm2_1', 'e2', 'z2', 's2',
         'c_a1', 'c_b1', 'c_a2', 'c_b2', 'c_t', 'a_a1', 'a_b1', 'a_a2', 'a_b2', 'a_t')
STRIDE = 13


def step_kernel(cfg, *refs):
    n, sl, rl, S, R, CM, CZ, H, D, HT, DT, OP, HP = cfg
    WM = H * D
    WT = HT * DT
    side = math.isqrt(n // 2)
    chunk = rl * OP // 2
    it = iter(refs)
    (m_ref, z_ref, mask_ref, rmask_ref, wb_hbm, wr_hbm, wro_hbm, wc_hbm, wco_hbm, wpi_hbm, wpo_hbm,
     wsb_hbm, ws_hbm, wso_hbm, web_hbm, we_hbm, weo_hbm) = [next(it) for _ in range(17)]
    m_out, z_out = next(it), next(it)
    wb, wr, wro, wc, wco, wpi, wpo, wsb, ws, wso, web, we, weo = weights = [next(it) for _ in range(13)]
    bias_f, biast_f = next(it), next(it)
    xz, qkvg, pbuf, vbuf = [next(it) for _ in range(4)]
    qvg, kbuf, gbuf, kmask, vmask = [next(it) for _ in range(5)]
    mrow, mcol, zb, znb = [next(it) for _ in range(4)]
    abuf, cbuf, abuf2, cbuf2, perm, obuf = [next(it) for _ in range(6)]
    mcolmask, seqmask, rmaskt, colmask, norm_ref = [next(it) for _ in range(5)]
    send = {}
    recv = {}
    for name in EXCHANGES:
        send[name] = next(it)
        recv[name] = next(it)
    send_sem, recv_sem, w_sem = next(it), next(it), next(it)
    hbm = [wb_hbm, wr_hbm, wro_hbm, wc_hbm, wco_hbm, wpi_hbm, wpo_hbm, wsb_hbm, ws_hbm, wso_hbm, web_hbm, we_hbm, weo_hbm]
    loads = [pltpu.make_async_copy(src, dst, w_sem.at[i]) for i, (src, dst) in enumerate(zip(hbm, weights))]
    for load in loads:
        load.start()
    (ld_wb, ld_wr, ld_wro, ld_wc, ld_wco, ld_wpi, ld_wpo, ld_wsb, ld_ws, ld_wso, ld_web, ld_we, ld_weo) = loads

    me = lax.axis_index('dap')
    barrier = pltpu.get_barrier_semaphore()

    @pl.loop(1, n)
    def _(k):
        pl.semaphore_signal(barrier, inc=1, device_id={'dap': lax.rem(me + k, n)}, device_id_type=MESH)

    core, px, py = me % 2, (me // 2) % side, me // (2 * side)

    def at(y, x, c):
        return {'dap': ((y % side) * side + x % side) * 2 + c % 2}

    def remote(flow, src, dst, device):
        f = FLOWS.index(flow)
        return pltpu.make_async_remote_copy(src_ref=src, dst_ref=dst, send_sem=send_sem.at[f], recv_sem=recv_sem.at[f], device_id=device, device_id_type=MESH)

    def wait_for(flow, sems, like):
        pltpu.make_async_copy(like, like, sems.at[FLOWS.index(flow)]).wait()

    def push(flow, src, dst, scatter):
        @pl.loop(1, n)
        def _(k):
            peer = lax.rem(me + k * STRIDE, n)
            remote(flow, src.at[peer] if scatter else src, dst.at[me], {'dap': peer}).start()
        dst[me] = src[me] if scatter else src[...]

    def target(flow):
        if flow[0] == 'm':
            return recv[flow[:2]].at[int(flow[3])]
        return recv[flow]

    def like(flow):
        if flow[1] != '_':
            return target(flow).at[pl.ds(0, n - 1)]
        dst, part = recv[flow[0]], flow[2:]
        rows = slice(0, chunk)
        if part == 't':
            return dst.at[:, :, 0]
        if part[1] == '1':
            return dst.at[0, pl.ds(0, side - 1), 0, rows]
        return dst.at[pl.ds(0, side - 1), :, 0, rows]

    def arrived(flow):
        wait_for(flow, recv_sem, like(flow))

    def spread(name, half):
        rows = slice(half * chunk, (half + 1) * chunk)
        dst = recv[name]
        dst[py, px, core, rows] = send[name][rows]
        for d in range(1, side):
            device = at(py, px + d, core) if half == 0 else at(py + d, px, core)
            remote(name + '_' + 'ab'[half] + '1', send[name].at[rows], dst.at[py, px, core, rows], device).start()

    def relay(name, half):
        arrived(name + '_' + 'ab'[half] + '1')
        rows = slice(half * chunk, (half + 1) * chunk)
        dst = recv[name]
        for d in range(1, side):
            if half == 0:
                part, device = dst.at[py, :, core, rows], at(py + d, px, core)
            else:
                part, device = dst.at[:, px, core, rows], at(py, px + d, core)
            remote(name + '_' + 'ab'[half] + '2', part, part, device).start()

    def share(name):
        arrived(name + '_a2')
        arrived(name + '_b2')
        part = recv[name].at[:, :, core]
        remote(name + '_t', part, part, at(py, px, core + 1)).start()

    eye = one_hot(R, R, lambda r: r)

    def pair_norm(zref):
        for i in range(rl):
            xz[:, i * R:(i + 1) * R] = norm_axis(zref[i].astype(F32), 0)

    def bias_block(name, w, heads):
        got = mm(w, xz[...]).astype(BF16).astype(F32)
        got = jnp.concatenate([got[:, i * R:(i + 1) * R] for i in range(rl)], axis=0).astype(BF16)
        padded = w.shape[0]
        if padded != heads:
            pack = one_hot(rl * heads, rl * padded, lambda r: (r // heads) * padded + r % heads)
            got = mm(pack, got).astype(BF16)
        send[name][...] = got
        push(name, send[name], recv[name], False)

    def bias_build(name, heads, group, dst, transpose):
        swap = swap_matrix(group * rl, heads)
        rows = group * rl

        @pl.loop(0, n // group)
        def _(g):
            got = mm(swap, recv[name][pl.ds(g * group, group)].reshape(rows * heads, R)) * LOG2E
            at = pl.ds(pl.multiple_of(g * rows, rows), rows)
            for h in range(heads):
                dst[h, at, :] = got[h * rows:(h + 1) * rows]
        if transpose:
            @pl.loop(0, heads)
            def _(h):
                dst[h] = dst[h].T

    def pair_project(w):
        got = mm(w, xz[...])
        for i in range(rl):
            qkvg[i] = got[:, i * R:(i + 1) * R].astype(BF16)

    def pair_attend(zref, wo, dst):
        scale = DT ** -0.5 * LOG2E

        @pl.loop(0, rl)
        def _(i):
            qt = qkvg[i, 0:WT]
            k = qkvg[i, WT:2 * WT].astype(F32).T.astype(BF16).reshape(R // 16, 16, WT)
            vt = qkvg[i, 2 * WT:3 * WT].reshape(WT // 16, 16, R)
            for h in range(HT):
                kh = (k * kmask[h][None]).reshape(R, WT)
                t = mm(kh, qt) * scale + biast_f[h]
                t = jnp.where(rmaskt[...] > 0, t, NEG)
                pbuf[h * R:(h + 1) * R, :] = softmax_cols(t)
                vbuf[:, h * R:(h + 1) * R] = (vt * vmask[h][None]).reshape(WT, R)
            o = mm(vbuf[...], pbuf[...])
            gated = (o * jax.nn.sigmoid(qkvg[i, 3 * WT:4 * WT].astype(F32))).astype(BF16)
            dst[i] = (zref[i].astype(F32) + mm(wo, gated)).astype(BF16)

    def pair_send(name):
        for i in range(rl):
            znb[i] = zb[i].astype(F32).T.astype(BF16)
        swap = one_hot(4 * rl * rl, 4 * rl * rl, lambda r: (r % rl) * (4 * rl) + r // rl)
        width = 4 * rl

        @pl.loop(0, n // 4)
        def _(g):
            got = znb[:, pl.ds(pl.multiple_of(g * width, width), width), :].reshape(rl * width, CZ)
            send[name][pl.ds(g * 4, 4)] = mm(swap, got).astype(BF16).reshape(4, rl * rl, CZ)
        push(name, send[name], recv[name], True)

    def pair_receive(name):
        rows = 8 * rl
        swap = one_hot(rows * rl, rows * rl, lambda r: ((r % rows) // rl) * (rl * rl) + (r // rows) * rl + r % rl)

        @pl.loop(0, n // 8)
        def _(g):
            got = mm(swap, recv[name][pl.ds(g * 8, 8)].reshape(rows * rl, CZ)).astype(BF16)
            at = pl.ds(pl.multiple_of(g * rows, rows), rows)
            for i in range(rl):
                znb[i, at, :] = got[i * rows:(i + 1) * rows]
        for i in range(rl):
            zb[i] = znb[i].astype(F32).T.astype(BF16)

    def outer_update(name, left, wo, zref, dst):
        swap = swap_matrix(4 * rl, 16)
        width = 4 * rl

        @pl.loop(0, n // 4)
        def _(g):
            for half in range(OP // 16):
                per = side // 2
                got = recv[name][g // per, pl.ds((g % per) * 2, 2)].reshape(width, OP, S)[:, half * 16:(half + 1) * 16].reshape(width * 16, S)
                perm[half * 16:(half + 1) * 16, pl.ds(pl.multiple_of(g * width, width), width), :] = mm(swap, got).astype(BF16).reshape(16, width, S)

        @pl.loop(0, OP // 2)
        def _(t):
            o = mm(left[...], perm[pl.ds(t * 2, 2)].reshape(2 * R, S), NT).astype(BF16)
            for u in range(2):
                at = pl.ds(pl.multiple_of((t * 2 + u) * OP, OP), OP)
                for i in range(rl):
                    obuf[at, i * R:(i + 1) * R] = o[i * OP:(i + 1) * OP, u * R:(u + 1) * R]
        upd = mm(wo, obuf[...])
        for i in range(rl):
            dst[i] = (zref[i].astype(F32) + upd[:, i * R:(i + 1) * R] * (1.0 / (1e-3 + norm_ref[i:i + 1, :]))).astype(BF16)

    def project(x, w, p):
        qvg[p, 0:WM] = mm(w[0:WM], x, NT).astype(BF16)
        kbuf[p] = mm(x, w[WM:2 * WM], NT).astype(BF16)
        qvg[p, WM:3 * WM] = mm(w[2 * WM:4 * WM], x, NT).astype(BF16)

    per_tile = 128 // D
    tile_lane = lax.broadcasted_iota(jnp.int32, (16, 128), 1) // D
    head_mask = [jnp.where(tile_lane == j, 1.0, 0.0).astype(BF16) for j in range(per_tile)]

    def attend(p, lo, size, mask, bias):
        scale = D ** -0.5 * LOG2E
        keys = slice(lo, lo + size)

        def logits(h, q):
            tile = (h // per_tile) * 128
            kt = kbuf[p, keys, tile:tile + 128].reshape(size // 16, 16, 128)
            kh = (kt * head_mask[h % per_tile][None]).reshape(size, 128)
            return mm(kh, qvg[p, tile:tile + 128, q:q + 128])
        blocks = [(h, q) for h in range(H) for q in range(lo, lo + size, 128)]
        ahead = logits(*blocks[0])
        for b, (h, q) in enumerate(blocks):
            t = ahead * scale
            if b + 1 < len(blocks):
                ahead = logits(*blocks[b + 1])
            if bias is not None:
                t = t + bias[h]
            t = jnp.where(mask > 0, t, NEG)
            o = mm(qvg[p, WM + h * D:WM + (h + 1) * D, keys], softmax_cols(t))
            g = qvg[p, 2 * WM + h * D:2 * WM + (h + 1) * D, q:q + 128].astype(F32)
            gbuf[h * D:(h + 1) * D, q:q + 128] = (o * jax.nn.sigmoid(g)).astype(BF16)

    def row_project(src, w):
        @pl.loop(0, sl // 2)
        def _(t):
            xf = src[pl.ds(2 * t, 2)].astype(F32).reshape(2 * R, CM)
            project(norm_axis(xf, 1), w, t)

    def row_attend(src, wo, bias, dst, lo, hi, after):
        @pl.loop(lo, hi)
        def _(t):
            for u in range(2):
                row = seqmask[pl.ds(2 * t + u, 1), :]
                mask = mm(eye, jnp.broadcast_to(row, (R, R)).astype(BF16), NT)
                attend(t, u * R, R, mask, bias)
            xf = src[pl.ds(2 * t, 2)].astype(F32).reshape(2 * R, CM)
            upd = mm(gbuf[...], wo[...], TN)
            dst[pl.ds(2 * t, 2)] = (xf + upd).astype(BF16).reshape(2, R, CM)
            after(t)

    def col_attention(w, wo, wp, a_dst, c_dst, after):
        @pl.loop(0, rl)
        def _(i):
            xf = mcol[i].astype(F32)
            project(norm_axis(xf, 1), w, 0)
            pick = jnp.where(lax.broadcasted_iota(jnp.int32, (R, R), 0) == me * rl + i, 1.0, 0.0).astype(BF16)
            attend(0, 0, S, mm(mcolmask[...], pick), None)
            y = (xf + mm(gbuf[...], wo[...], TN)).astype(BF16)
            mcol[i] = y
            x = norm_axis(y.astype(F32), 1)
            half = (mm(wp, x, NT) * colmask[pl.ds(i, 1), :]).astype(BF16)
            at = pl.ds(pl.multiple_of(i * OP, OP), OP)
            a_dst[at, :] = half[0:OP]
            c_dst[at, :] = half[OP:2 * OP]
            after(i)

    sh = sl // 2
    order = one_hot(S, S, lambda r: ((r % (n * sh)) // sh) * sl + (r // (n * sh)) * sh + r % sh)
    maskf = mm(order, mask_ref[...].astype(F32).astype(BF16)).astype(BF16)
    mcolmask[...] = maskf
    seqmask[...] = mask_ref[pl.ds(pl.multiple_of(me * sl, sl), sl), :].astype(F32)
    rmaskt[...] = mm(eye, jnp.broadcast_to(rmask_ref[...].astype(F32), (R, R)).astype(BF16), NT)
    pick = jnp.where(lax.broadcasted_iota(jnp.int32, (8, R), 1) == lax.broadcasted_iota(jnp.int32, (8, R), 0) + me * rl, 1.0, 0.0).astype(BF16)
    colmask[...] = mm(pick, maskf, NT)
    norm_ref[...] = mm(colmask[...].astype(BF16), maskf)
    for h in range(HT):
        kmask[h] = jnp.where(lax.broadcasted_iota(jnp.int32, (16, WT), 1) % HT == h, 1.0, 0.0).astype(BF16)
        vmask[h] = jnp.where(lax.broadcasted_iota(jnp.int32, (16, R), 0) % HT == h, 1.0, 0.0).astype(BF16)

    pair_norm(z_ref)
    ld_wb.wait()
    pl.semaphore_wait(barrier, n - 1)
    bias_block('b1', wb[0], H)
    ld_wr.wait()
    row_project(m_ref, wr.at[0])
    ld_wro.wait()
    arrived('b1')
    bias_build('b1', H, 8, bias_f, True)

    per = 16 // rl
    split = one_hot(16 * sh, 16 * sh, lambda r: (r % sh) * 16 + r // sh)

    def send_rows(half):
        @pl.loop(0, R // 16)
        def _(g):
            got = mrow[half * sh:(half + 1) * sh, pl.ds(pl.multiple_of(g * 16, 16), 16), :].reshape(sh * 16, CM)
            send['m1'][half, pl.ds(g * per, per)] = mm(split, got).astype(BF16).reshape(per, rl * sh, CM)
        push('m1_%d' % half, send['m1'].at[half], recv['m1'].at[half], True)

    def after_row(t):
        for half in range(2):
            pl.when(t == (half + 1) * (sl // 4) - 1)(functools.partial(send_rows, half))
    row_attend(m_ref, wro.at[0], bias_f, mrow, 0, sl // 2, after_row)

    ld_wc.wait()
    ld_wco.wait()
    ld_wpi.wait()
    join = one_hot(8 * rl * sh, 8 * rl * sh, lambda r: ((r % (8 * sh)) // sh) * (rl * sh) + (r // (8 * sh)) * sh + r % sh)
    for half in range(2):
        arrived('m1_%d' % half)

        @pl.loop(0, n // 8)
        def _(g):
            got = mm(join, recv['m1'][half, pl.ds(g * 8, 8)].reshape(8 * rl * sh, CM)).astype(BF16)
            at = pl.ds(pl.multiple_of(half * n * sh + g * 8 * sh, 8 * sh), 8 * sh)
            for i in range(rl):
                mcol[i, at, :] = got[i * 8 * sh:(i + 1) * 8 * sh]

    def after_first(i):
        pl.when(i == rl // 2 - 1)(lambda: spread('c', 0))
    col_attention(wc.at[0], wco.at[0], wpi[0], abuf, send['c'], after_first)
    spread('c', 1)
    relay('c', 0)

    back = one_hot(8 * rl * sh, 8 * rl * sh, lambda r: ((r % (4 * sh)) // sh) * (8 * sh) + (r // (4 * sh)) * sh + r % sh)

    def send_cols(pair):
        @pl.loop(0, n // 8)
        def _(g):
            got = jnp.concatenate([mcol[2 * pair + u, pl.ds(pl.multiple_of(half * n * sh + g * 8 * sh, 8 * sh), 8 * sh), :] for u in range(2) for half in range(2)], axis=0)
            send['m2'][pair, pl.ds(g * 8, 8)] = mm(back, got).astype(BF16).reshape(8, 4 * sh, CM)
        push('m2_%d' % pair, send['m2'].at[pair], recv['m2'].at[pair], True)

    def after_second(i):
        @pl.when(i == 0)
        def _():
            relay('c', 1)

        @pl.when(i == 1)
        def _():
            spread('a', 0)
            send_cols(0)

        @pl.when(i == 2)
        def _():
            share('c')
    col_attention(wc.at[1], wco.at[1], wpi[1], send['a'], cbuf2, after_second)
    spread('a', 1)
    relay('a', 0)

    for load in (ld_wpo, ld_wsb, ld_ws, ld_wso, ld_web, ld_we, ld_weo):
        load.wait()
    arrived('c_t')
    outer_update('c', abuf, wpo[0], z_ref, zb)
    pair_norm(zb)
    bias_block('s1', wsb[0], HT)
    relay('a', 1)
    send_cols(1)
    pair_project(ws[0])
    arrived('s1')
    bias_build('s1', HT, 4, biast_f, True)
    pair_attend(zb, wso[0], zb)
    pair_send('z1')
    pair_norm(zb)
    bias_block('e1', web[0], HT)
    share('a')
    arrived('m2_0')
    arrived('m2_1')
    unsplit = one_hot(16 * sl, 16 * sl, lambda r: ((r % 4) // 2) * (8 * sl) + ((r % 16) // 4) * (2 * sl) + (r % 2) * sl + r // 16)

    @pl.loop(0, R // 16)
    def _(g):
        got = jnp.concatenate([recv['m2'][pair, pl.ds(g * per, per)].reshape(8 * sl, CM) for pair in range(2)], axis=0)
        mrow[:, pl.ds(pl.multiple_of(g * 16, 16), 16), :] = mm(unsplit, got).astype(BF16).reshape(sl, 16, CM)
    row_project(mrow, wr.at[1])
    arrived('z1')
    pair_receive('z1')
    pair_norm(zb)
    pair_project(we[0])
    arrived('e1')
    bias_build('e1', HT, 4, biast_f, False)
    pair_attend(zb, weo[0], zb)

    pair_norm(zb)
    bias_block('b2', wb[1], H)
    arrived('a_t')
    outer_update('a', cbuf2, wpo[1], zb, zb)
    pair_norm(zb)
    bias_block('e2', web[1], HT)
    pair_project(we[1])
    arrived('b2')
    bias_build('b2', H, 8, bias_f, False)
    row_attend(mrow, wro.at[1], bias_f, m_out, 0, sl // 4, lambda t: None)
    arrived('e2')
    bias_build('e2', HT, 4, biast_f, True)
    pair_attend(zb, weo[1], zb)
    pair_send('z2')
    pair_norm(zb)
    bias_block('s2', wsb[1], HT)
    row_attend(mrow, wro.at[1], bias_f, m_out, sl // 4, sl // 2, lambda t: None)
    arrived('z2')
    pair_receive('z2')
    pair_norm(zb)
    pair_project(ws[1])
    arrived('s2')
    bias_build('s2', HT, 4, biast_f, False)
    pair_attend(zb, wso[1], z_out)
    for flow in FLOWS:
        wait_for(flow, send_sem, like(flow))


def solution(mesh):
    n = mesh.shape['dap']

    def local_step(m, z, mask, rmask, w_row_bias, w_row_in, w_row_out, w_col_in, w_col_out, w_opm_in, w_opm_out, w_ts_bias, w_ts_in, w_ts_out, w_te_bias, w_te_in, w_te_out):
        sl, R, CM = m.shape
        rl, _, CZ = z.shape
        S = mask.shape[0]
        H, D = w_row_in.shape[3:]
        HT, DT = w_ts_in.shape[3:]
        OP = w_opm_in.shape[3]
        HP = -(-H // 8) * 8
        WM, WT = H * D, HT * DT
        zt = z.transpose(0, 2, 1)
        wb = jnp.pad(w_row_bias.transpose(0, 2, 1), ((0, 0), (0, HP - H), (0, 0)))
        wr = w_row_in.transpose(0, 2, 3, 4, 1).reshape(2, 4 * WM, CM)
        wc = w_col_in.transpose(0, 2, 3, 4, 1).reshape(2, 4 * WM, CM)
        wro = w_row_out.reshape(2, WM, CM)
        wco = w_col_out.reshape(2, WM, CM)
        wpi = w_opm_in.transpose(0, 2, 3, 1).reshape(2, 2 * OP, CM)
        wpo = jnp.stack([w_opm_out[0].transpose(2, 1, 0).reshape(CZ, OP * OP), w_opm_out[1].transpose(2, 0, 1).reshape(CZ, OP * OP)])
        wsb = w_ts_bias.transpose(0, 2, 1)
        web = w_te_bias.transpose(0, 2, 1)
        ws = w_ts_in.transpose(0, 2, 4, 3, 1).reshape(2, 4 * WT, CZ)
        we = w_te_in.transpose(0, 2, 4, 3, 1).reshape(2, 4 * WT, CZ)
        wso = w_ts_out.transpose(0, 3, 2, 1).reshape(2, CZ, WT)
        weo = w_te_out.transpose(0, 3, 2, 1).reshape(2, CZ, WT)
        weights = [wb, wr, wro, wc, wco, wpi, wpo, wsb, ws, wso, web, we, weo]

        def vm(shape, dtype=BF16):
            return pltpu.VMEM(shape, dtype)
        scratch = [vm(w.shape) for w in weights]
        scratch += [vm((H, R, R), F32), vm((HT, R, R), F32)]
        scratch += [vm((CZ, rl * R)), vm((rl, 4 * WT, R)), vm((HT * R, R)), vm((WT, HT * R))]
        scratch += [vm((sl // 2, 3 * WM, S)), vm((sl // 2, S, WM)), vm((WM, S)), vm((HT, 16, WT)), vm((HT, 16, R))]
        scratch += [vm((sl, R, CM)), vm((rl, S, CM)), vm((rl, CZ, R)), vm((rl, R, CZ))]
        scratch += [vm((rl * OP, S))] * 4 + [vm((OP, R, S)), vm((OP * OP, rl * R))]
        scratch += [vm((S, R)), vm((sl, R), F32), vm((R, R), F32), vm((8, S), F32), vm((8, R), F32)]
        side = math.isqrt(n // 2)
        bias_row, bias_tri = (rl * H, R), (rl * HT, R)
        shapes = {'b1': bias_row, 'b2': bias_row, 's1': bias_tri, 'e1': bias_tri, 'e2': bias_tri, 's2': bias_tri,
                  'c': (rl * OP, S), 'a': (rl * OP, S), 'm1': (rl * sl // 2, CM), 'm2': (rl * sl // 2, CM), 'z1': (rl * rl, CZ), 'z2': (rl * rl, CZ)}
        for name in EXCHANGES:
            shape = shapes[name]
            if name in 'ac':
                scratch += [vm(shape), vm((side, side, 2) + shape)]
            elif name[0] == 'm':
                scratch += [vm((2, n) + shape), vm((2, n) + shape)]
            else:
                scratch += [vm((n,) + shape if name[0] == 'z' else shape), vm((n,) + shape)]
        scratch += [pltpu.SemaphoreType.DMA((len(FLOWS),)), pltpu.SemaphoreType.DMA((len(FLOWS),)), pltpu.SemaphoreType.DMA((len(weights),))]
        cfg = (n, sl, rl, S, R, CM, CZ, H, D, HT, DT, OP, HP)
        vmem = pl.BlockSpec(memory_space=pltpu.VMEM)
        hbm = pl.BlockSpec(memory_space=pl.ANY)
        m_new, z_new = pl.pallas_call(
            functools.partial(step_kernel, cfg),
            out_shape=[jax.ShapeDtypeStruct(m.shape, BF16), jax.ShapeDtypeStruct(zt.shape, BF16)],
            in_specs=[vmem] * 4 + [hbm] * len(weights),
            out_specs=[vmem, vmem],
            scratch_shapes=scratch,
            compiler_params=pltpu.CompilerParams(collective_id=0, has_side_effects=True, vmem_limit_bytes=60 * 2**20),
            name='evoformer',
        )(m, zt, mask, rmask.reshape(1, R), *weights)
        return m_new, z_new.transpose(0, 2, 1)

    in_specs = (P(('data', 'dap')), P(('data', 'dap')), P('data'), P('data')) + (P(),) * 13
    out_specs = (P(('data', 'dap')), P(('data', 'dap')))
    return jax.shard_map(local_step, mesh=mesh, in_specs=in_specs, out_specs=out_specs, check_vma=False)
```

time: 237 us -> 159 us (0.67)
  Pallas kernels: 227 us -> 150 us
    pallas_call x1, Pallas kernels: 227 us -> 150 us  [local_step(): pl.pallas_call(functools.partial(step_kernel, cfg), out_shape=[jax.ShapeD...]
where the time goes in v2:
time: 159 us
  Pallas kernels  150 us (94%)
  local copies, waits for them, and re-layouts  7.8 us (5%)
    pallas_call x1, Pallas kernels, local_step(): pl.pallas_call(functools.partial(step_kernel, cfg), out_shape=[jax.ShapeD...  150 us

profile of v2, /device:TPU:97, one launch (start us, length us, event | category | flops | bytes accessed | tf_op | source)
XLA Modules:
  0.0 159.1 jit_solution(15628419315646141208)
XLA Ops:
  0.6 1.5 slice_bitcast_fusion
  2.2 0.3 copy.25
  2.4 0.3 copy.26
  2.7 0.0 copy-start
  2.7 0.3 copy.27
  3.0 0.0 copy-start.1
  3.0 0.0 copy-start.3
  3.0 1.1 pad_maximum_fusion.refs_10_
  4.1 0.0 copy-done
  4.1 1.0 copy.28.refs_13_
  5.1 0.0 copy-done.1
  5.1 1.0 copy.29.refs_16_
  6.1 0.0 copy-done.3
  6.1 0.6 pad.4.refs_4_
  6.7 149.5 %evoformer.1 = (bf16[8,128,384]{2,1,0:T(8,128)(2,1)}, bf16[4,288,128]{2,1,0:T(8,128)(2,1)}) custom-call(bf16[8,128,384]{2,1,0:T(8,128)(2,1)} %refs_0_.1, bf16[4,288,128]{2,1,0:T(8,128)(2,1)} %bitcast.51, s32[256,128]{1,0:T(8,128)} %refs_2_.1, s32[1,128]{1,0:T(1,128)} %bitcast.57, bf16[2,16,288]{2,1,0:T(8,128)(2,1)} %pad.4.refs_4_, ...), custom_call_target="tpu_custom_call" | custom-call | tf_op jit(solution)/shard_map/evoformer/pallas_call | solution.py:517
  156.3 0.0 copy-start.2
  156.3 2.1 %copy.34 = bf16[8,128,384]{2,1,0:T(8,128)(2,1)} copy(bf16[8,128,384]{2,1,0:T(8,128)(2,1)} %get-tuple-element.10) | data formatting | bytes 1572864
  158.4 0.0 copy-done.2
  158.4 0.7 copy.35
  (1 shorter events, 0.0 us)
Async XLA Ops:
  2.7 1.4 copy-start
  3.0 2.1 %copy-start.1 = (bf16[2,8,36,288]{3,1,2,0:T(8,128)(2,1)S(1)}, bf16[2,8,36,288]{3,1,2,0:T(8,128)(2,1)}, u32[]{:S(2)}) copy-start(bf16[2,8,36,288]{3,1,2,0:T(8,128)(2,1)} %param.33) | copy-start | bytes 995332
  3.0 3.1 %copy-start.3 = (bf16[2,288,12]{1,0,2:T(2,128)(2,1)S(1)}, bf16[2,288,12]{1,0,2:T(2,128)(2,1)}, u32[]{:S(2)}) copy-start(bf16[2,288,12]{1,0,2:T(2,128)(2,1)} %param.21) | copy-start | bytes 41476
  156.3 2.1 %copy-start.2 = (bf16[4,288,128]{2,1,0:T(8,128)(2,1)S(1)}, bf16[4,288,128]{2,1,0:T(8,128)(2,1)}, u32[]{:S(2)}) copy-start(bf16[4,288,128]{2,1,0:T(8,128)(2,1)} %get-tuple-element.5) | copy-start | bytes 884740

commit v3 on v2

--- a/solution.py
+++ b/solution.py
@@ -62,6 +62,7 @@
      wsb_hbm, ws_hbm, wso_hbm, web_hbm, we_hbm, weo_hbm) = [next(it) for _ in range(17)]
     m_out, z_out = next(it), next(it)
     wb, wr, wro, wc, wco, wpi, wpo, wsb, ws, wso, web, we, weo = weights = [next(it) for _ in range(13)]
+    wtmp, wpot, wsot, weot = [next(it) for _ in range(4)]
     bias_f, biast_f = next(it), next(it)
     xz, qkvg, pbuf, vbuf = [next(it) for _ in range(4)]
     qvg, kbuf, gbuf, kmask, vmask = [next(it) for _ in range(5)]
@@ -157,6 +158,10 @@
             xz[:, i * R:(i + 1) * R] = norm_axis(zref[i].astype(F32), 0)
 
     def bias_block(name, w, heads):
+        bias_pack(name, w, heads)
+        push(name, send[name], recv[name], False)
+
+    def bias_pack(name, w, heads):
         got = mm(w, xz[...]).astype(BF16).astype(F32)
         got = jnp.concatenate([got[:, i * R:(i + 1) * R] for i in range(rl)], axis=0).astype(BF16)
         padded = w.shape[0]
@@ -164,7 +169,6 @@
             pack = one_hot(rl * heads, rl * padded, lambda r: (r // heads) * padded + r % heads)
             got = mm(pack, got).astype(BF16)
         send[name][...] = got
-        push(name, send[name], recv[name], False)
 
     def bias_build(name, heads, group, dst, transpose):
         swap = swap_matrix(group * rl, heads)
@@ -288,7 +292,7 @@
             xf = src[pl.ds(2 * t, 2)].astype(F32).reshape(2 * R, CM)
             project(norm_axis(xf, 1), w, t)
 
-    def row_attend(src, wo, bias, dst, lo, hi, after):
+    def row_attend(src, wo, bias, dst, lo, hi):
         @pl.loop(lo, hi)
         def _(t):
             for u in range(2):
@@ -298,12 +302,11 @@
             xf = src[pl.ds(2 * t, 2)].astype(F32).reshape(2 * R, CM)
             upd = mm(gbuf[...], wo[...], TN)
             dst[pl.ds(2 * t, 2)] = (xf + upd).astype(BF16).reshape(2, R, CM)
-            after(t)
-
-    def col_attention(w, wo, wp, a_dst, c_dst, after):
+
+    def col_attention(load, w, wo, wp, a_dst, c_dst, after):
         @pl.loop(0, rl)
         def _(i):
-            xf = mcol[i].astype(F32)
+            xf = load(i)
             project(norm_axis(xf, 1), w, 0)
             pick = jnp.where(lax.broadcasted_iota(jnp.int32, (R, R), 0) == me * rl + i, 1.0, 0.0).astype(BF16)
             attend(0, 0, S, mm(mcolmask[...], pick), None)
@@ -316,9 +319,7 @@
             c_dst[at, :] = half[OP:2 * OP]
             after(i)
 
-    sh = sl // 2
-    order = one_hot(S, S, lambda r: ((r % (n * sh)) // sh) * sl + (r // (n * sh)) * sh + r % sh)
-    maskf = mm(order, mask_ref[...].astype(F32).astype(BF16)).astype(BF16)
+    maskf = mask_ref[...].astype(F32).astype(BF16)
     mcolmask[...] = maskf
     seqmask[...] = mask_ref[pl.ds(pl.multiple_of(me * sl, sl), sl), :].astype(F32)
     rmaskt[...] = mm(eye, jnp.broadcast_to(rmask_ref[...].astype(F32), (R, R)).astype(BF16), NT)
@@ -339,48 +340,52 @@
     arrived('b1')
     bias_build('b1', H, 8, bias_f, True)
 
+    row_attend(m_ref, wro.at[0], bias_f, mrow, 0, sl // 2)
+
     per = 16 // rl
-    split = one_hot(16 * sh, 16 * sh, lambda r: (r % sh) * 16 + r // sh)
-
-    def send_rows(half):
-        @pl.loop(0, R // 16)
-        def _(g):
-            got = mrow[half * sh:(half + 1) * sh, pl.ds(pl.multiple_of(g * 16, 16), 16), :].reshape(sh * 16, CM)
-            send['m1'][half, pl.ds(g * per, per)] = mm(split, got).astype(BF16).reshape(per, rl * sh, CM)
-        push('m1_%d' % half, send['m1'].at[half], recv['m1'].at[half], True)
-
-    def after_row(t):
-        for half in range(2):
-            pl.when(t == (half + 1) * (sl // 4) - 1)(functools.partial(send_rows, half))
-    row_attend(m_ref, wro.at[0], bias_f, mrow, 0, sl // 2, after_row)
+    split = one_hot(16 * sl, 16 * sl, lambda r: (r % sl) * 16 + ((r // (2 * sl)) % per) * rl + (r // (2 * sl * per)) * 2 + (r // sl) % 2)
+
+    @pl.loop(0, R // 16)
+    def _(g):
+        got = mrow[:, pl.ds(pl.multiple_of(g * 16, 16), 16), :].reshape(sl * 16, CM)
+        got = mm(split, got).astype(BF16).reshape(2, per, 2 * sl, CM)
+        for pair in range(2):
+            send['m1'][pair, pl.ds(g * per, per)] = got[pair]
+    for pair in range(2):
+        push('m1_%d' % pair, send['m1'].at[pair], recv['m1'].at[pair], True)
+
+    for load in (ld_wpo, ld_wsb, ld_ws, ld_wso, ld_web, ld_we, ld_weo):
+        load.wait()
+    swap = swap_matrix(16, 16)
+    for p in range(OP // 16):
+        for q in range(OP // 16):
+            got = wpo[0].reshape(OP, OP, CZ)[p * 16:(p + 1) * 16, q * 16:(q + 1) * 16].reshape(256, CZ)
+            wtmp[q * 16:(q + 1) * 16, p * 16:(p + 1) * 16, :] = mm(swap, got).astype(BF16).reshape(16, 16, CZ)
+    wpot[0] = wtmp[...].reshape(OP * OP, CZ).astype(F32).T.astype(BF16)
+    wpot[1] = wpo[1].astype(F32).T.astype(BF16)
+    for b in range(2):
+        wsot[b] = wso[b].astype(F32).T.astype(BF16)
+        weot[b] = weo[b].astype(F32).T.astype(BF16)
 
     ld_wc.wait()
     ld_wco.wait()
     ld_wpi.wait()
-    join = one_hot(8 * rl * sh, 8 * rl * sh, lambda r: ((r % (8 * sh)) // sh) * (rl * sh) + (r // (8 * sh)) * sh + r % sh)
-    for half in range(2):
-        arrived('m1_%d' % half)
-
-        @pl.loop(0, n // 8)
-        def _(g):
-            got = mm(join, recv['m1'][half, pl.ds(g * 8, 8)].reshape(8 * rl * sh, CM)).astype(BF16)
-            at = pl.ds(pl.multiple_of(half * n * sh + g * 8 * sh, 8 * sh), 8 * sh)
-            for i in range(rl):
-                mcol[i, at, :] = got[i * 8 * sh:(i + 1) * 8 * sh]
+    arrived('m1_0')
+
+    def load_first(i):
+        pl.when(i == 2)(lambda: arrived('m1_1'))
+        got = recv['m1'][i // 2].astype(F32)
+        return jnp.where(i % 2 == 0, got[:, 0:sl], got[:, sl:2 * sl]).reshape(S, CM)
 
     def after_first(i):
         pl.when(i == rl // 2 - 1)(lambda: spread('c', 0))
-    col_attention(wc.at[0], wco.at[0], wpi[0], abuf, send['c'], after_first)
+    col_attention(load_first, wc.at[0], wco.at[0], wpi[0], abuf, send['c'], after_first)
     spread('c', 1)
     relay('c', 0)
 
-    back = one_hot(8 * rl * sh, 8 * rl * sh, lambda r: ((r % (4 * sh)) // sh) * (8 * sh) + (r // (4 * sh)) * sh + r % sh)
-
     def send_cols(pair):
-        @pl.loop(0, n // 8)
-        def _(g):
-            got = jnp.concatenate([mcol[2 * pair + u, pl.ds(pl.multiple_of(half * n * sh + g * 8 * sh, 8 * sh), 8 * sh), :] for u in range(2) for half in range(2)], axis=0)
-            send['m2'][pair, pl.ds(g * 8, 8)] = mm(back, got).astype(BF16).reshape(8, 4 * sh, CM)
+        got = [mcol[2 * pair + u].astype(F32).reshape(n, sl, CM) for u in range(2)]
+        send['m2'][pair] = jnp.concatenate(got, axis=1).astype(BF16)
         push('m2_%d' % pair, send['m2'].at[pair], recv['m2'].at[pair], True)
 
     def after_second(i):
@@ -396,26 +401,40 @@
         @pl.when(i == 2)
         def _():
             share('c')
-    col_attention(wc.at[1], wco.at[1], wpi[1], send['a'], cbuf2, after_second)
+    col_attention(lambda i: mcol[i].astype(F32), wc.at[1], wco.at[1], wpi[1], send['a'], cbuf2, after_second)
     spread('a', 1)
-    relay('a', 0)
-
-    for load in (ld_wpo, ld_wsb, ld_ws, ld_wso, ld_web, ld_we, ld_weo):
-        load.wait()
+
     arrived('c_t')
-    outer_update('c', abuf, wpo[0], z_ref, zb)
+    outer_update('c', abuf, wpot[0], z_ref, zb)
     pair_norm(zb)
     bias_block('s1', wsb[0], HT)
-    relay('a', 1)
-    send_cols(1)
     pair_project(ws[0])
     arrived('s1')
+    relay('a', 0)
+    relay('a', 1)
     bias_build('s1', HT, 4, biast_f, True)
-    pair_attend(zb, wso[0], zb)
+    pair_attend(zb, wsot[0], zb)
     pair_send('z1')
     pair_norm(zb)
     bias_block('e1', web[0], HT)
     share('a')
+    arrived('z1')
+    pair_receive('z1')
+    pair_norm(zb)
+    pair_project(we[0])
+    arrived('e1')
+    send_cols(1)
+    bias_build('e1', HT, 4, biast_f, False)
+    pair_attend(zb, weot[0], zb)
+
+    pair_norm(zb)
+    bias_pack('b2', wb[1], H)
+    arrived('a_t')
+    outer_update('a', cbuf2, wpot[1], zb, zb)
+    pair_norm(zb)
+    bias_block('e2', web[1], HT)
+    push('b2', send['b2'], recv['b2'], False)
+    pair_project(we[1])
     arrived('m2_0')
     arrived('m2_1')
     unsplit = one_hot(16 * sl, 16 * sl, lambda r: ((r % 4) // 2) * (8 * sl) + ((r % 16) // 4) * (2 * sl) + (r % 2) * sl + r // 16)
@@ -425,38 +444,22 @@
         got = jnp.concatenate([recv['m2'][pair, pl.ds(g * per, per)].reshape(8 * sl, CM) for pair in range(2)], axis=0)
         mrow[:, pl.ds(pl.multiple_of(g * 16, 16), 16), :] = mm(unsplit, got).astype(BF16).reshape(sl, 16, CM)
     row_project(mrow, wr.at[1])
-    arrived('z1')
-    pair_receive('z1')
-    pair_norm(zb)
-    pair_project(we[0])
-    arrived('e1')
-    bias_build('e1', HT, 4, biast_f, False)
-    pair_attend(zb, weo[0], zb)
-
-    pair_norm(zb)
-    bias_block('b2', wb[1], H)
-    arrived('a_t')
-    outer_update('a', cbuf2, wpo[1], zb, zb)
-    pair_norm(zb)
-    bias_block('e2', web[1], HT)
-    pair_project(we[1])
+    arrived('e2')
+    bias_build('e2', HT, 4, biast_f, True)
+    pair_attend(zb, weot[1], zb)
+    pair_send('z2')
+    pair_norm(zb)
+    bias_block('s2', wsb[1], HT)
     arrived('b2')
     bias_build('b2', H, 8, bias_f, False)
-    row_attend(mrow, wro.at[1], bias_f, m_out, 0, sl // 4, lambda t: None)
-    arrived('e2')
-    bias_build('e2', HT, 4, biast_f, True)
-    pair_attend(zb, weo[1], zb)
-    pair_send('z2')
-    pair_norm(zb)
-    bias_block('s2', wsb[1], HT)
-    row_attend(mrow, wro.at[1], bias_f, m_out, sl // 4, sl // 2, lambda t: None)
+    row_attend(mrow, wro.at[1], bias_f, m_out, 0, sl // 2)
     arrived('z2')
     pair_receive('z2')
     pair_norm(zb)
     pair_project(ws[1])
     arrived('s2')
     bias_build('s2', HT, 4, biast_f, False)
-    pair_attend(zb, wso[1], z_out)
+    pair_attend(zb, wsot[1], z_out)
     for flow in FLOWS:
         wait_for(flow, send_sem, like(flow))
 
@@ -480,18 +483,19 @@
         wro = w_row_out.reshape(2, WM, CM)
         wco = w_col_out.reshape(2, WM, CM)
         wpi = w_opm_in.transpose(0, 2, 3, 1).reshape(2, 2 * OP, CM)
-        wpo = jnp.stack([w_opm_out[0].transpose(2, 1, 0).reshape(CZ, OP * OP), w_opm_out[1].transpose(2, 0, 1).reshape(CZ, OP * OP)])
+        wpo = w_opm_out.reshape(2, OP * OP, CZ)
         wsb = w_ts_bias.transpose(0, 2, 1)
         web = w_te_bias.transpose(0, 2, 1)
         ws = w_ts_in.transpose(0, 2, 4, 3, 1).reshape(2, 4 * WT, CZ)
         we = w_te_in.transpose(0, 2, 4, 3, 1).reshape(2, 4 * WT, CZ)
-        wso = w_ts_out.transpose(0, 3, 2, 1).reshape(2, CZ, WT)
-        weo = w_te_out.transpose(0, 3, 2, 1).reshape(2, CZ, WT)
+        wso = w_ts_out.transpose(0, 2, 1, 3).reshape(2, WT, CZ)
+        weo = w_te_out.transpose(0, 2, 1, 3).reshape(2, WT, CZ)
         weights = [wb, wr, wro, wc, wco, wpi, wpo, wsb, ws, wso, web, we, weo]
 
         def vm(shape, dtype=BF16):
             return pltpu.VMEM(shape, dtype)
         scratch = [vm(w.shape) for w in weights]
+        scratch += [vm((OP, OP, CZ)), vm((2, CZ, OP * OP)), vm((2, CZ, WT)), vm((2, CZ, WT))]
         scratch += [vm((H, R, R), F32), vm((HT, R, R), F32)]
         scratch += [vm((CZ, rl * R)), vm((rl, 4 * WT, R)), vm((HT * R, R)), vm((WT, HT * R))]
         scratch += [vm((sl // 2, 3 * WM, S)), vm((sl // 2, S, WM)), vm((WM, S)), vm((HT, 16, WT)), vm((HT, 16, R))]

time: 159 us -> 152 us (0.956)
  local copies, waits for them, and re-layouts: 7.8 us -> 4.2 us
  Pallas kernels: 150 us -> 147 us
    pallas_call x1, Pallas kernels: 150 us -> 147 us  [local_step(): pl.pallas_call(functools.partial(step_kernel, cfg), out_shape=[jax.ShapeD...]
    reshape x2 -> x0, local copies, waits for them, and re-layouts: 1.99 us -> none  [the longest x1 1 us: local_step(): weo = w_te_out.transpose(0, 3, 2, 1).reshape(2, CZ, WT)]
    transpose x2 -> x0, local copies, waits for them, and re-layouts: 1.79 us -> none  [local_step(): w_opm_out[0].transpose(2, 1, 0).reshape(CZ, OP * OP)]
    unnamed x11 -> x5, local copies, waits for them, and re-layouts: 2.88 us -> 3.58 us
where the time goes in v3:
time: 152 us
  Pallas kernels  147 us (97%)
  local copies, waits for them, and re-layouts  4.2 us (3%)
    pallas_call x1, Pallas kernels, local_step(): pl.pallas_call(functools.partial(step_kernel, cfg), out_shape=[jax.ShapeD...  147 us
    unnamed x5, local copies, waits for them, and re-layouts  3.58 us

profile of v3, /device:TPU:97, one launch (start us, length us, event | category | flops | bytes accessed | tf_op | source)
XLA Modules:
  0.0 151.6 jit_solution(2028098841547580562)
XLA Ops:
  0.6 0.7 copy.21
  1.4 0.6 pad.4.refs_4_
  2.0 146.7 %evoformer.1 = (bf16[8,128,384]{2,1,0:T(8,128)(2,1)}, bf16[4,288,128]{2,1,0:T(8,128)(2,1)}) custom-call(bf16[8,128,384]{2,1,0:T(8,128)(2,1)} %refs_0_.1, bf16[4,288,128]{2,1,0:T(8,128)(2,1)} %bitcast.41, s32[256,128]{1,0:T(8,128)} %refs_2_.1, s32[1,128]{1,0:T(1,128)} %bitcast.47, bf16[2,16,288]{2,1,0:T(8,128)(2,1)} %pad.4.refs_4_, ...), custom_call_target="tpu_custom_call" | custom-call | tf_op jit(solution)/shard_map/evoformer/pallas_call | solution.py:521
  148.7 0.0 copy-start
  148.7 2.1 %copy.24 = bf16[8,128,384]{2,1,0:T(8,128)(2,1)} copy(bf16[8,128,384]{2,1,0:T(8,128)(2,1)} %get-tuple-element.8) | data formatting | bytes 1572864
  150.8 0.0 copy-done
  150.8 0.7 copy.25
Async XLA Ops:
  148.7 2.1 %copy-start = (bf16[4,288,128]{2,1,0:T(8,128)(2,1)S(1)}, bf16[4,288,128]{2,1,0:T(8,128)(2,1)}, u32[]{:S(2)}) copy-start(bf16[4,288,128]{2,1,0:T(8,128)(2,1)} %get-tuple-element.5) | copy-start | bytes 884740

commit v4 on v3

--- a/solution.py
+++ b/solution.py
@@ -174,15 +174,12 @@
         swap = swap_matrix(group * rl, heads)
         rows = group * rl
 
-        @pl.loop(0, n // group)
-        def _(g):
-            got = mm(swap, recv[name][pl.ds(g * group, group)].reshape(rows * heads, R)) * LOG2E
-            at = pl.ds(pl.multiple_of(g * rows, rows), rows)
+        for g in range(n // group):
+            got = mm(swap, recv[name][g * group:(g + 1) * group].reshape(rows * heads, R)) * LOG2E
             for h in range(heads):
-                dst[h, at, :] = got[h * rows:(h + 1) * rows]
+                dst[h, g * rows:(g + 1) * rows, :] = got[h * rows:(h + 1) * rows]
         if transpose:
-            @pl.loop(0, heads)
-            def _(h):
+            for h in range(heads):
                 dst[h] = dst[h].T
 
     def pair_project(w):
@@ -214,22 +211,19 @@
         swap = one_hot(4 * rl * rl, 4 * rl * rl, lambda r: (r % rl) * (4 * rl) + r // rl)
         width = 4 * rl
 
-        @pl.loop(0, n // 4)
-        def _(g):
-            got = znb[:, pl.ds(pl.multiple_of(g * width, width), width), :].reshape(rl * width, CZ)
-            send[name][pl.ds(g * 4, 4)] = mm(swap, got).astype(BF16).reshape(4, rl * rl, CZ)
+        for g in range(n // 4):
+            got = znb[:, g * width:(g + 1) * width, :].reshape(rl * width, CZ)
+            send[name][g * 4:(g + 1) * 4] = mm(swap, got).astype(BF16).reshape(4, rl * rl, CZ)
         push(name, send[name], recv[name], True)
 
     def pair_receive(name):
         rows = 8 * rl
         swap = one_hot(rows * rl, rows * rl, lambda r: ((r % rows) // rl) * (rl * rl) + (r // rows) * rl + r % rl)
 
-        @pl.loop(0, n // 8)
-        def _(g):
-            got = mm(swap, recv[name][pl.ds(g * 8, 8)].reshape(rows * rl, CZ)).astype(BF16)
-            at = pl.ds(pl.multiple_of(g * rows, rows), rows)
+        for g in range(n // 8):
+            got = mm(swap, recv[name][g * 8:(g + 1) * 8].reshape(rows * rl, CZ)).astype(BF16)
             for i in range(rl):
-                znb[i, at, :] = got[i * rows:(i + 1) * rows]
+                znb[i, g * rows:(g + 1) * rows, :] = got[i * rows:(i + 1) * rows]
         for i in range(rl):
             zb[i] = znb[i].astype(F32).T.astype(BF16)
 
@@ -237,20 +231,16 @@
         swap = swap_matrix(4 * rl, 16)
         width = 4 * rl
 
-        @pl.loop(0, n // 4)
-        def _(g):
+        per_y = side // 2
+        for g in range(n // 4):
             for half in range(OP // 16):
-                per = side // 2
-                got = recv[name][g // per, pl.ds((g % per) * 2, 2)].reshape(width, OP, S)[:, half * 16:(half + 1) * 16].reshape(width * 16, S)
-                perm[half * 16:(half + 1) * 16, pl.ds(pl.multiple_of(g * width, width), width), :] = mm(swap, got).astype(BF16).reshape(16, width, S)
-
-        @pl.loop(0, OP // 2)
-        def _(t):
-            o = mm(left[...], perm[pl.ds(t * 2, 2)].reshape(2 * R, S), NT).astype(BF16)
+                got = recv[name][g // per_y, (g % per_y) * 2:(g % per_y) * 2 + 2].reshape(width, OP, S)[:, half * 16:(half + 1) * 16].reshape(width * 16, S)
+                perm[half * 16:(half + 1) * 16, g * width:(g + 1) * width, :] = mm(swap, got).astype(BF16).reshape(16, width, S)
+        for t in range(OP // 2):
+            o = mm(left[...], perm[t * 2:t * 2 + 2].reshape(2 * R, S), NT).astype(BF16)
             for u in range(2):
-                at = pl.ds(pl.multiple_of((t * 2 + u) * OP, OP), OP)
                 for i in range(rl):
-                    obuf[at, i * R:(i + 1) * R] = o[i * OP:(i + 1) * OP, u * R:(u + 1) * R]
+                    obuf[(t * 2 + u) * OP:(t * 2 + u + 1) * OP, i * R:(i + 1) * R] = o[i * OP:(i + 1) * OP, u * R:(u + 1) * R]
         upd = mm(wo, obuf[...])
         for i in range(rl):
             dst[i] = (zref[i].astype(F32) + upd[:, i * R:(i + 1) * R] * (1.0 / (1e-3 + norm_ref[i:i + 1, :]))).astype(BF16)
@@ -268,23 +258,39 @@
         scale = D ** -0.5 * LOG2E
         keys = slice(lo, lo + size)
 
-        def logits(h, q):
+        def query(h, q):
+            j = h % per_tile
+            parts = [qvg[p, h * D:(h + 1) * D, q:q + 128]]
+            if j:
+                parts.insert(0, jnp.zeros((j * D, 128), BF16))
+            if j + 1 < per_tile:
+                parts.append(jnp.zeros(((per_tile - 1 - j) * D, 128), BF16))
+            return jnp.concatenate(parts, axis=0)
+
+        def logits(group):
+            h, q = group[0]
             tile = (h // per_tile) * 128
-            kt = kbuf[p, keys, tile:tile + 128].reshape(size // 16, 16, 128)
-            kh = (kt * head_mask[h % per_tile][None]).reshape(size, 128)
-            return mm(kh, qvg[p, tile:tile + 128, q:q + 128])
+            if len(group) == 1:
+                kt = kbuf[p, keys, tile:tile + 128].reshape(size // 16, 16, 128)
+                kh = (kt * head_mask[h % per_tile][None]).reshape(size, 128)
+                return mm(kh, qvg[p, tile:tile + 128, q:q + 128])
+            return mm(kbuf[p, keys, tile:tile + 128], jnp.concatenate([query(h, q) for h, q in group], axis=1))
         blocks = [(h, q) for h in range(H) for q in range(lo, lo + size, 128)]
-        ahead = logits(*blocks[0])
-        for b, (h, q) in enumerate(blocks):
-            t = ahead * scale
-            if b + 1 < len(blocks):
-                ahead = logits(*blocks[b + 1])
-            if bias is not None:
-                t = t + bias[h]
-            t = jnp.where(mask > 0, t, NEG)
-            o = mm(qvg[p, WM + h * D:WM + (h + 1) * D, keys], softmax_cols(t))
-            g = qvg[p, 2 * WM + h * D:2 * WM + (h + 1) * D, q:q + 128].astype(F32)
-            gbuf[h * D:(h + 1) * D, q:q + 128] = (o * jax.nn.sigmoid(g)).astype(BF16)
+        step = size // 128
+        groups = [blocks[b:b + step] for b in range(0, len(blocks), step)]
+        ahead = logits(groups[0])
+        for b, group in enumerate(groups):
+            now = ahead
+            if b + 1 < len(groups):
+                ahead = logits(groups[b + 1])
+            for u, (h, q) in enumerate(group):
+                t = now[:, u * 128:(u + 1) * 128] * scale
+                if bias is not None:
+                    t = t + bias[h]
+                t = jnp.where(mask > 0, t, NEG)
+                o = mm(qvg[p, WM + h * D:WM + (h + 1) * D, keys], softmax_cols(t))
+                g = qvg[p, 2 * WM + h * D:2 * WM + (h + 1) * D, q:q + 128].astype(F32)
+                gbuf[h * D:(h + 1) * D, q:q + 128] = (o * jax.nn.sigmoid(g)).astype(BF16)
 
     def row_project(src, w):
         @pl.loop(0, sl // 2)
@@ -345,12 +351,10 @@
     per = 16 // rl
     split = one_hot(16 * sl, 16 * sl, lambda r: (r % sl) * 16 + ((r // (2 * sl)) % per) * rl + (r // (2 * sl * per)) * 2 + (r // sl) % 2)
 
-    @pl.loop(0, R // 16)
-    def _(g):
-        got = mrow[:, pl.ds(pl.multiple_of(g * 16, 16), 16), :].reshape(sl * 16, CM)
-        got = mm(split, got).astype(BF16).reshape(2, per, 2 * sl, CM)
+    for g in range(R // 16):
+        got = mm(split, mrow[:, g * 16:(g + 1) * 16, :].reshape(sl * 16, CM)).astype(BF16).reshape(2, per, 2 * sl, CM)
         for pair in range(2):
-            send['m1'][pair, pl.ds(g * per, per)] = got[pair]
+            send['m1'][pair, g * per:(g + 1) * per] = got[pair]
     for pair in range(2):
         push('m1_%d' % pair, send['m1'].at[pair], recv['m1'].at[pair], True)
 
@@ -439,10 +443,9 @@
     arrived('m2_1')
     unsplit = one_hot(16 * sl, 16 * sl, lambda r: ((r % 4) // 2) * (8 * sl) + ((r % 16) // 4) * (2 * sl) + (r % 2) * sl + r // 16)
 
-    @pl.loop(0, R // 16)
-    def _(g):
-        got = jnp.concatenate([recv['m2'][pair, pl.ds(g * per, per)].reshape(8 * sl, CM) for pair in range(2)], axis=0)
-        mrow[:, pl.ds(pl.multiple_of(g * 16, 16), 16), :] = mm(unsplit, got).astype(BF16).reshape(sl, 16, CM)
+    for g in range(R // 16):
+        got = jnp.concatenate([recv['m2'][pair, g * per:(g + 1) * per].reshape(8 * sl, CM) for pair in range(2)], axis=0)
+        mrow[:, g * 16:(g + 1) * 16, :] = mm(unsplit, got).astype(BF16).reshape(sl, 16, CM)
     row_project(mrow, wr.at[1])
     arrived('e2')
     bias_build('e2', HT, 4, biast_f, True)

time: 152 us -> 128 us (0.84)
  Pallas kernels: 147 us -> 123 us
    pallas_call x1, Pallas kernels: 147 us -> 123 us  [local_step(): pl.pallas_call(functools.partial(step_kernel, cfg), out_shape=[jax.ShapeD...]
where the time goes in v4:
time: 128 us
  Pallas kernels  123 us (96%)
  local copies, waits for them, and re-layouts  4.2 us (3%)
    pallas_call x1, Pallas kernels, local_step(): pl.pallas_call(functools.partial(step_kernel, cfg), out_shape=[jax.ShapeD...  123 us
    unnamed x5, local copies, waits for them, and re-layouts  3.58 us

profile of v4, /device:TPU:97, one launch (start us, length us, event | category | flops | bytes accessed | tf_op | source)
XLA Modules:
  0.0 127.7 jit_solution(8784121586366145519)
XLA Ops:
  0.6 0.7 copy.21
  1.4 0.6 pad.4.refs_4_
  2.0 122.8 %evoformer.1 = (bf16[8,128,384]{2,1,0:T(8,128)(2,1)}, bf16[4,288,128]{2,1,0:T(8,128)(2,1)}) custom-call(bf16[8,128,384]{2,1,0:T(8,128)(2,1)} %refs_0_.1, bf16[4,288,128]{2,1,0:T(8,128)(2,1)} %bitcast.41, s32[256,128]{1,0:T(8,128)} %refs_2_.1, s32[1,128]{1,0:T(1,128)} %bitcast.47, bf16[2,16,288]{2,1,0:T(8,128)(2,1)} %pad.4.refs_4_, ...), custom_call_target="tpu_custom_call" | custom-call | tf_op jit(solution)/shard_map/evoformer/pallas_call | solution.py:524
  124.8 0.0 copy-start
  124.8 2.1 %copy.24 = bf16[8,128,384]{2,1,0:T(8,128)(2,1)} copy(bf16[8,128,384]{2,1,0:T(8,128)(2,1)} %get-tuple-element.8) | data formatting | bytes 1572864
  126.9 0.0 copy-done
  126.9 0.7 copy.25
Async XLA Ops:
  124.8 2.1 %copy-start = (bf16[4,288,128]{2,1,0:T(8,128)(2,1)S(1)}, bf16[4,288,128]{2,1,0:T(8,128)(2,1)}, u32[]{:S(2)}) copy-start(bf16[4,288,128]{2,1,0:T(8,128)(2,1)} %get-tuple-element.5) | copy-start | bytes 884740

commit v5 on v4

--- a/solution.py
+++ b/solution.py
@@ -55,6 +55,8 @@
     n, sl, rl, S, R, CM, CZ, H, D, HT, DT, OP, HP = cfg
     WM = H * D
     WT = HT * DT
+    DP = -(-DT // 16) * 16
+    WP = HT * DP
     side = math.isqrt(n // 2)
     chunk = rl * OP // 2
     it = iter(refs)
@@ -64,8 +66,8 @@
     wb, wr, wro, wc, wco, wpi, wpo, wsb, ws, wso, web, we, weo = weights = [next(it) for _ in range(13)]
     wtmp, wpot, wsot, weot = [next(it) for _ in range(4)]
     bias_f, biast_f = next(it), next(it)
-    xz, qkvg, pbuf, vbuf = [next(it) for _ in range(4)]
-    qvg, kbuf, gbuf, kmask, vmask = [next(it) for _ in range(5)]
+    xz, qkvg, gpair, wsp, wep = [next(it) for _ in range(5)]
+    qvg, kbuf, gbuf = [next(it) for _ in range(3)]
     mrow, mcol, zb, znb = [next(it) for _ in range(4)]
     abuf, cbuf, abuf2, cbuf2, perm, obuf = [next(it) for _ in range(6)]
     mcolmask, seqmask, rmaskt, colmask, norm_ref = [next(it) for _ in range(5)]
@@ -192,18 +194,20 @@
 
         @pl.loop(0, rl)
         def _(i):
-            qt = qkvg[i, 0:WT]
-            k = qkvg[i, WT:2 * WT].astype(F32).T.astype(BF16).reshape(R // 16, 16, WT)
-            vt = qkvg[i, 2 * WT:3 * WT].reshape(WT // 16, 16, R)
+            def part(f, h):
+                return qkvg[i, f * WP + h * DP:f * WP + (h + 1) * DP]
+
+            def logits(h):
+                return mm(part(1, h).astype(F32).T.astype(BF16), part(0, h))
+            ahead = logits(0)
             for h in range(HT):
-                kh = (k * kmask[h][None]).reshape(R, WT)
-                t = mm(kh, qt) * scale + biast_f[h]
+                t = ahead * scale + biast_f[h]
+                if h + 1 < HT:
+                    ahead = logits(h + 1)
                 t = jnp.where(rmaskt[...] > 0, t, NEG)
-                pbuf[h * R:(h + 1) * R, :] = softmax_cols(t)
-                vbuf[:, h * R:(h + 1) * R] = (vt * vmask[h][None]).reshape(WT, R)
-            o = mm(vbuf[...], pbuf[...])
-            gated = (o * jax.nn.sigmoid(qkvg[i, 3 * WT:4 * WT].astype(F32))).astype(BF16)
-            dst[i] = (zref[i].astype(F32) + mm(wo, gated)).astype(BF16)
+                o = mm(part(2, h), softmax_cols(t))
+                gpair[h * DP:(h + 1) * DP, :] = (o * jax.nn.sigmoid(part(3, h).astype(F32))).astype(BF16)
+            dst[i] = (zref[i].astype(F32) + mm(wo, gpair[...])).astype(BF16)
 
     def pair_send(name):
         for i in range(rl):
@@ -332,9 +336,6 @@
     pick = jnp.where(lax.broadcasted_iota(jnp.int32, (8, R), 1) == lax.broadcasted_iota(jnp.int32, (8, R), 0) + me * rl, 1.0, 0.0).astype(BF16)
     colmask[...] = mm(pick, maskf, NT)
     norm_ref[...] = mm(colmask[...].astype(BF16), maskf)
-    for h in range(HT):
-        kmask[h] = jnp.where(lax.broadcasted_iota(jnp.int32, (16, WT), 1) % HT == h, 1.0, 0.0).astype(BF16)
-        vmask[h] = jnp.where(lax.broadcasted_iota(jnp.int32, (16, R), 0) % HT == h, 1.0, 0.0).astype(BF16)
 
     pair_norm(z_ref)
     ld_wb.wait()
@@ -343,23 +344,7 @@
     ld_wr.wait()
     row_project(m_ref, wr.at[0])
     ld_wro.wait()
-    arrived('b1')
-    bias_build('b1', H, 8, bias_f, True)
-
-    row_attend(m_ref, wro.at[0], bias_f, mrow, 0, sl // 2)
-
-    per = 16 // rl
-    split = one_hot(16 * sl, 16 * sl, lambda r: (r % sl) * 16 + ((r // (2 * sl)) % per) * rl + (r // (2 * sl * per)) * 2 + (r // sl) % 2)
-
-    for g in range(R // 16):
-        got = mm(split, mrow[:, g * 16:(g + 1) * 16, :].reshape(sl * 16, CM)).astype(BF16).reshape(2, per, 2 * sl, CM)
-        for pair in range(2):
-            send['m1'][pair, g * per:(g + 1) * per] = got[pair]
-    for pair in range(2):
-        push('m1_%d' % pair, send['m1'].at[pair], recv['m1'].at[pair], True)
-
-    for load in (ld_wpo, ld_wsb, ld_ws, ld_wso, ld_web, ld_we, ld_weo):
-        load.wait()
+    ld_wpo.wait()
     swap = swap_matrix(16, 16)
     for p in range(OP // 16):
         for q in range(OP // 16):
@@ -367,9 +352,29 @@
             wtmp[q * 16:(q + 1) * 16, p * 16:(p + 1) * 16, :] = mm(swap, got).astype(BF16).reshape(16, 16, CZ)
     wpot[0] = wtmp[...].reshape(OP * OP, CZ).astype(F32).T.astype(BF16)
     wpot[1] = wpo[1].astype(F32).T.astype(BF16)
-    for b in range(2):
-        wsot[b] = wso[b].astype(F32).T.astype(BF16)
-        weot[b] = weo[b].astype(F32).T.astype(BF16)
+    arrived('b1')
+    bias_build('b1', H, 8, bias_f, True)
+
+    row_attend(m_ref, wro.at[0], bias_f, mrow, 0, sl // 2)
+
+    per = 16 // rl
+    split = one_hot(16 * sl, 16 * sl, lambda r: (r % sl) * 16 + ((r // (2 * sl)) % per) * rl + (r // (2 * sl * per)) * 2 + (r // sl) % 2)
+
+    for g in range(R // 16):
+        got = mm(split, mrow[:, g * 16:(g + 1) * 16, :].reshape(sl * 16, CM)).astype(BF16).reshape(2, per, 2 * sl, CM)
+        for pair in range(2):
+            send['m1'][pair, g * per:(g + 1) * per] = got[pair]
+    for pair in range(2):
+        push('m1_%d' % pair, send['m1'].at[pair], recv['m1'].at[pair], True)
+
+    for load in (ld_wsb, ld_ws, ld_wso, ld_web, ld_we, ld_weo):
+        load.wait()
+    heads = one_hot(WP, WT, lambda r: jnp.where(r % DP < DT, (r % DP) * HT + r // DP, -1))
+    for raw, out, turned, dst in ((ws, wso, wsp, wsot), (we, weo, wep, weot)):
+        for b in range(2):
+            for f in range(4):
+                turned[b, f * WP:(f + 1) * WP] = mm(heads, raw[b, f * WT:(f + 1) * WT]).astype(BF16)
+            dst[b] = mm(heads, out[b]).T.astype(BF16)
 
     ld_wc.wait()
     ld_wco.wait()
@@ -412,7 +417,7 @@
     outer_update('c', abuf, wpot[0], z_ref, zb)
     pair_norm(zb)
     bias_block('s1', wsb[0], HT)
-    pair_project(ws[0])
+    pair_project(wsp[0])
     arrived('s1')
     relay('a', 0)
     relay('a', 1)
@@ -425,7 +430,7 @@
     arrived('z1')
     pair_receive('z1')
     pair_norm(zb)
-    pair_project(we[0])
+    pair_project(wep[0])
     arrived('e1')
     send_cols(1)
     bias_build('e1', HT, 4, biast_f, False)
@@ -438,7 +443,7 @@
     pair_norm(zb)
     bias_block('e2', web[1], HT)
     push('b2', send['b2'], recv['b2'], False)
-    pair_project(we[1])
+    pair_project(wep[1])
     arrived('m2_0')
     arrived('m2_1')
     unsplit = one_hot(16 * sl, 16 * sl, lambda r: ((r % 4) // 2) * (8 * sl) + ((r % 16) // 4) * (2 * sl) + (r % 2) * sl + r // 16)
@@ -459,7 +464,7 @@
     arrived('z2')
     pair_receive('z2')
     pair_norm(zb)
-    pair_project(ws[1])
+    pair_project(wsp[1])
     arrived('s2')
     bias_build('s2', HT, 4, biast_f, False)
     pair_attend(zb, wsot[1], z_out)
@@ -479,6 +484,7 @@
         OP = w_opm_in.shape[3]
         HP = -(-H // 8) * 8
         WM, WT = H * D, HT * DT
+        WP = HT * -(-DT // 16) * 16
         zt = z.transpose(0, 2, 1)
         wb = jnp.pad(w_row_bias.transpose(0, 2, 1), ((0, 0), (0, HP - H), (0, 0)))
         wr = w_row_in.transpose(0, 2, 3, 4, 1).reshape(2, 4 * WM, CM)
@@ -498,10 +504,10 @@
         def vm(shape, dtype=BF16):
             return pltpu.VMEM(shape, dtype)
         scratch = [vm(w.shape) for w in weights]
-        scratch += [vm((OP, OP, CZ)), vm((2, CZ, OP * OP)), vm((2, CZ, WT)), vm((2, CZ, WT))]
+        scratch += [vm((OP, OP, CZ)), vm((2, CZ, OP * OP)), vm((2, CZ, WP)), vm((2, CZ, WP))]
         scratch += [vm((H, R, R), F32), vm((HT, R, R), F32)]
-        scratch += [vm((CZ, rl * R)), vm((rl, 4 * WT, R)), vm((HT * R, R)), vm((WT, HT * R))]
-        scratch += [vm((sl // 2, 3 * WM, S)), vm((sl // 2, S, WM)), vm((WM, S)), vm((HT, 16, WT)), vm((HT, 16, R))]
+        scratch += [vm((CZ, rl * R)), vm((rl, 4 * WP, R)), vm((WP, R)), vm((2, 4 * WP, CZ)), vm((2, 4 * WP, CZ))]
+        scratch += [vm((sl // 2, 3 * WM, S)), vm((sl // 2, S, WM)), vm((WM, S))]
         scratch += [vm((sl, R, CM)), vm((rl, S, CM)), vm((rl, CZ, R)), vm((rl, R, CZ))]
         scratch += [vm((rl * OP, S))] * 4 + [vm((OP, R, S)), vm((OP * OP, rl * R))]
         scratch += [vm((S, R)), vm((sl, R), F32), vm((R, R), F32), vm((8, S), F32), vm((8, R), F32)]

time: 128 us -> 126 us (0.984)
  Pallas kernels: 123 us -> 121 us
    pallas_call x1, Pallas kernels: 123 us -> 121 us  [local_step(): pl.pallas_call(functools.partial(step_kernel, cfg), out_shape=[jax.ShapeD...]
where the time goes in v5:
time: 126 us
  Pallas kernels  121 us (96%)
  local copies, waits for them, and re-layouts  4.2 us (3%)
    pallas_call x1, Pallas kernels, local_step(): pl.pallas_call(functools.partial(step_kernel, cfg), out_shape=[jax.ShapeD...  121 us
    unnamed x5, local copies, waits for them, and re-layouts  3.58 us

profile of v5, /device:TPU:97, one launch (start us, length us, event | category | flops | bytes accessed | tf_op | source)
XLA Modules:
  0.0 126.2 jit_solution(6625372650499231843)
XLA Ops:
  0.6 0.7 copy.21
  1.4 0.6 pad.4.refs_4_
  2.0 121.4 %evoformer.1 = (bf16[8,128,384]{2,1,0:T(8,128)(2,1)}, bf16[4,288,128]{2,1,0:T(8,128)(2,1)}) custom-call(bf16[8,128,384]{2,1,0:T(8,128)(2,1)} %refs_0_.1, bf16[4,288,128]{2,1,0:T(8,128)(2,1)} %bitcast.41, s32[256,128]{1,0:T(8,128)} %refs_2_.1, s32[1,128]{1,0:T(1,128)} %bitcast.47, bf16[2,16,288]{2,1,0:T(8,128)(2,1)} %pad.4.refs_4_, ...), custom_call_target="tpu_custom_call" | custom-call | tf_op jit(solution)/shard_map/evoformer/pallas_call | solution.py:530
  123.4 0.0 copy-start
  123.4 2.1 %copy.24 = bf16[8,128,384]{2,1,0:T(8,128)(2,1)} copy(bf16[8,128,384]{2,1,0:T(8,128)(2,1)} %get-tuple-element.8) | data formatting | bytes 1572864
  125.5 0.0 copy-done
  125.5 0.7 copy.25
Async XLA Ops:
  123.4 2.1 %copy-start = (bf16[4,288,128]{2,1,0:T(8,128)(2,1)S(1)}, bf16[4,288,128]{2,1,0:T(8,128)(2,1)}, u32[]{:S(2)}) copy-start(bf16[4,288,128]{2,1,0:T(8,128)(2,1)} %get-tuple-element.5) | copy-start | bytes 884740

commit v6 on v5

--- a/solution.py
+++ b/solution.py
@@ -192,8 +192,7 @@
     def pair_attend(zref, wo, dst):
         scale = DT ** -0.5 * LOG2E
 
-        @pl.loop(0, rl)
-        def _(i):
+        def row(i, u):
             def part(f, h):
                 return qkvg[i, f * WP + h * DP:f * WP + (h + 1) * DP]
 
@@ -206,8 +205,13 @@
                     ahead = logits(h + 1)
                 t = jnp.where(rmaskt[...] > 0, t, NEG)
                 o = mm(part(2, h), softmax_cols(t))
-                gpair[h * DP:(h + 1) * DP, :] = (o * jax.nn.sigmoid(part(3, h).astype(F32))).astype(BF16)
-            dst[i] = (zref[i].astype(F32) + mm(wo, gpair[...])).astype(BF16)
+                gpair[u, h * DP:(h + 1) * DP, :] = (o * jax.nn.sigmoid(part(3, h).astype(F32))).astype(BF16)
+            dst[i] = (zref[i].astype(F32) + mm(wo, gpair[u])).astype(BF16)
+
+        @pl.loop(0, rl // 2)
+        def _(t):
+            row(2 * t, 0)
+            row(2 * t + 1, 1)
 
     def pair_send(name):
         for i in range(rl):
@@ -248,6 +252,10 @@
         upd = mm(wo, obuf[...])
         for i in range(rl):
             dst[i] = (zref[i].astype(F32) + upd[:, i * R:(i + 1) * R] * (1.0 / (1e-3 + norm_ref[i:i + 1, :]))).astype(BF16)
+
+    def row_bias_weight(b):
+        got = wb[:, b, :].astype(F32)
+        return jnp.concatenate([got, jnp.zeros((HP - H, CZ), F32)], axis=0).astype(BF16)
 
     def project(x, w, p):
         qvg[p, 0:WM] = mm(w[0:WM], x, NT).astype(BF16)
@@ -340,7 +348,7 @@
     pair_norm(z_ref)
     ld_wb.wait()
     pl.semaphore_wait(barrier, n - 1)
-    bias_block('b1', wb[0], H)
+    bias_block('b1', row_bias_weight(0), H)
     ld_wr.wait()
     row_project(m_ref, wr.at[0])
     ld_wro.wait()
@@ -437,7 +445,7 @@
     pair_attend(zb, weot[0], zb)
 
     pair_norm(zb)
-    bias_pack('b2', wb[1], H)
+    bias_pack('b2', row_bias_weight(1), H)
     arrived('a_t')
     outer_update('a', cbuf2, wpot[1], zb, zb)
     pair_norm(zb)
@@ -486,7 +494,7 @@
         WM, WT = H * D, HT * DT
         WP = HT * -(-DT // 16) * 16
         zt = z.transpose(0, 2, 1)
-        wb = jnp.pad(w_row_bias.transpose(0, 2, 1), ((0, 0), (0, HP - H), (0, 0)))
+        wb = w_row_bias.transpose(2, 0, 1)
         wr = w_row_in.transpose(0, 2, 3, 4, 1).reshape(2, 4 * WM, CM)
         wc = w_col_in.transpose(0, 2, 3, 4, 1).reshape(2, 4 * WM, CM)
         wro = w_row_out.reshape(2, WM, CM)
@@ -506,7 +514,7 @@
         scratch = [vm(w.shape) for w in weights]
         scratch += [vm((OP, OP, CZ)), vm((2, CZ, OP * OP)), vm((2, CZ, WP)), vm((2, CZ, WP))]
         scratch += [vm((H, R, R), F32), vm((HT, R, R), F32)]
-        scratch += [vm((CZ, rl * R)), vm((rl, 4 * WP, R)), vm((WP, R)), vm((2, 4 * WP, CZ)), vm((2, 4 * WP, CZ))]
+        scratch += [vm((CZ, rl * R)), vm((rl, 4 * WP, R)), vm((2, WP, R)), vm((2, 4 * WP, CZ)), vm((2, 4 * WP, CZ))]
         scratch += [vm((sl // 2, 3 * WM, S)), vm((sl // 2, S, WM)), vm((WM, S))]
         scratch += [vm((sl, R, CM)), vm((rl, S, CM)), vm((rl, CZ, R)), vm((rl, R, CZ))]
         scratch += [vm((rl * OP, S))] * 4 + [vm((OP, R, S)), vm((OP * OP, rl * R))]

time: 126 us -> 124 us (0.984)
  local copies, waits for them, and re-layouts: 4.2 us -> 2.85 us
    unnamed x5 -> x4, local copies, waits for them, and re-layouts: 3.58 us -> 2.85 us
where the time goes in v6:
time: 124 us
  Pallas kernels  121 us (98%)
  local copies, waits for them, and re-layouts  2.85 us (2%)
    pallas_call x1, Pallas kernels, local_step(): pl.pallas_call(functools.partial(step_kernel, cfg), out_shape=[jax.ShapeD...  121 us
    unnamed x4, local copies, waits for them, and re-layouts  2.85 us

profile of v6, /device:TPU:97, one launch (start us, length us, event | category | flops | bytes accessed | tf_op | source)
XLA Modules:
  0.0 124.3 jit_solution(5179497717338717709)
XLA Ops:
  0.6 120.8 %evoformer.1 = (bf16[8,128,384]{2,1,0:T(8,128)(2,1)}, bf16[4,288,128]{2,1,0:T(8,128)(2,1)}) custom-call(bf16[8,128,384]{2,1,0:T(8,128)(2,1)} %refs_0_.1, bf16[4,288,128]{2,1,0:T(8,128)(2,1)} %bitcast.39, s32[256,128]{1,0:T(8,128)} %refs_2_.1, s32[1,128]{1,0:T(1,128)} %bitcast.45, bf16[12,2,288]{2,1,0:T(2,128)(2,1)} %bitcast.42, ...), custom_call_target="tpu_custom_call" | custom-call | tf_op jit(solution)/shard_map/evoformer/pallas_call | solution.py:538
  121.4 0.0 copy-start
  121.4 2.1 %copy.21 = bf16[8,128,384]{2,1,0:T(8,128)(2,1)} copy(bf16[8,128,384]{2,1,0:T(8,128)(2,1)} %get-tuple-element.8) | data formatting | bytes 1572864
  123.6 0.0 copy-done
  123.6 0.7 copy.22
Async XLA Ops:
  121.4 2.1 %copy-start = (bf16[4,288,128]{2,1,0:T(8,128)(2,1)S(1)}, bf16[4,288,128]{2,1,0:T(8,128)(2,1)}, u32[]{:S(2)}) copy-start(bf16[4,288,128]{2,1,0:T(8,128)(2,1)} %get-tuple-element.5) | copy-start | bytes 884740

commit v7 on v6

--- a/solution.py
+++ b/solution.py
@@ -1,4 +1,5 @@
 import functools
+import itertools
 import math
 
 import jax
@@ -48,7 +49,6 @@
 EXCHANGES = ('b1', 'm1', 'c', 's1', 'z1', 'e1', 'b2', 'a', 'm2', 'e2', 'z2', 's2')
 FLOWS = ('b1', 'm1_0', 'm1_1', 's1', 'z1', 'e1', 'b2', 'm2_0', 'm2_1', 'e2', 'z2', 's2',
          'c_a1', 'c_b1', 'c_a2', 'c_b2', 'c_t', 'a_a1', 'a_b1', 'a_a2', 'a_b2', 'a_t')
-STRIDE = 13
 
 
 def step_kernel(cfg, *refs):
@@ -68,7 +68,7 @@
     bias_f, biast_f = next(it), next(it)
     xz, qkvg, gpair, wsp, wep = [next(it) for _ in range(5)]
     qvg, kbuf, gbuf = [next(it) for _ in range(3)]
-    mrow, mcol, zb, znb = [next(it) for _ in range(4)]
+    mrow, mcol, zb, znb, mfinal = [next(it) for _ in range(5)]
     abuf, cbuf, abuf2, cbuf2, perm, obuf = [next(it) for _ in range(6)]
     mcolmask, seqmask, rmaskt, colmask, norm_ref = [next(it) for _ in range(5)]
     send = {}
@@ -92,6 +92,14 @@
 
     core, px, py = me % 2, (me // 2) % side, me // (2 * side)
 
+    rows_of = [(py + d) % side * (2 * side) for d in range(side)]
+    chips_of = [(px + d) % side * 2 for d in range(side)]
+    cores_of = [core, 1 - core]
+
+    def hops(offset):
+        return sum(min(d, side - d) for d in offset[:2])
+    offsets = sorted(itertools.product(range(side), range(side), range(2)), key=hops)[:0:-1]
+
     def at(y, x, c):
         return {'dap': ((y % side) * side + x % side) * 2 + c % 2}
 
@@ -103,9 +111,8 @@
         pltpu.make_async_copy(like, like, sems.at[FLOWS.index(flow)]).wait()
 
     def push(flow, src, dst, scatter):
-        @pl.loop(1, n)
-        def _(k):
-            peer = lax.rem(me + k * STRIDE, n)
+        for dy, dx, dc in offsets:
+            peer = rows_of[dy] + chips_of[dx] + cores_of[dc]
             remote(flow, src.at[peer] if scatter else src, dst.at[me], {'dap': peer}).start()
         dst[me] = src[me] if scatter else src[...]
 
@@ -206,7 +213,7 @@
                 t = jnp.where(rmaskt[...] > 0, t, NEG)
                 o = mm(part(2, h), softmax_cols(t))
                 gpair[u, h * DP:(h + 1) * DP, :] = (o * jax.nn.sigmoid(part(3, h).astype(F32))).astype(BF16)
-            dst[i] = (zref[i].astype(F32) + mm(wo, gpair[u])).astype(BF16)
+            dst[i] = (zref[i].astype(F32) + mm(wo, gpair[u])).astype(dst.dtype)
 
         @pl.loop(0, rl // 2)
         def _(t):
@@ -319,7 +326,7 @@
                 attend(t, u * R, R, mask, bias)
             xf = src[pl.ds(2 * t, 2)].astype(F32).reshape(2 * R, CM)
             upd = mm(gbuf[...], wo[...], TN)
-            dst[pl.ds(2 * t, 2)] = (xf + upd).astype(BF16).reshape(2, R, CM)
+            dst[pl.ds(2 * t, 2)] = (xf + upd).astype(dst.dtype).reshape(2, R, CM)
 
     def col_attention(load, w, wo, wp, a_dst, c_dst, after):
         @pl.loop(0, rl)
@@ -468,7 +475,9 @@
     bias_block('s2', wsb[1], HT)
     arrived('b2')
     bias_build('b2', H, 8, bias_f, False)
-    row_attend(mrow, wro.at[1], bias_f, m_out, 0, sl // 2)
+    row_attend(mrow, wro.at[1], bias_f, mfinal, 0, sl // 2)
+    store = pltpu.make_async_copy(mfinal, m_out, w_sem.at[0])
+    store.start()
     arrived('z2')
     pair_receive('z2')
     pair_norm(zb)
@@ -476,6 +485,7 @@
     arrived('s2')
     bias_build('s2', HT, 4, biast_f, False)
     pair_attend(zb, wsot[1], z_out)
+    store.wait()
     for flow in FLOWS:
         wait_for(flow, send_sem, like(flow))
 
@@ -516,7 +526,7 @@
         scratch += [vm((H, R, R), F32), vm((HT, R, R), F32)]
         scratch += [vm((CZ, rl * R)), vm((rl, 4 * WP, R)), vm((2, WP, R)), vm((2, 4 * WP, CZ)), vm((2, 4 * WP, CZ))]
         scratch += [vm((sl // 2, 3 * WM, S)), vm((sl // 2, S, WM)), vm((WM, S))]
-        scratch += [vm((sl, R, CM)), vm((rl, S, CM)), vm((rl, CZ, R)), vm((rl, R, CZ))]
+        scratch += [vm((sl, R, CM)), vm((rl, S, CM)), vm((rl, CZ, R)), vm((rl, R, CZ)), vm((sl, R, CM), F32)]
         scratch += [vm((rl * OP, S))] * 4 + [vm((OP, R, S)), vm((OP * OP, rl * R))]
         scratch += [vm((S, R)), vm((sl, R), F32), vm((R, R), F32), vm((8, S), F32), vm((8, R), F32)]
         side = math.isqrt(n // 2)
@@ -537,14 +547,14 @@
         hbm = pl.BlockSpec(memory_space=pl.ANY)
         m_new, z_new = pl.pallas_call(
             functools.partial(step_kernel, cfg),
-            out_shape=[jax.ShapeDtypeStruct(m.shape, BF16), jax.ShapeDtypeStruct(zt.shape, BF16)],
+            out_shape=[jax.ShapeDtypeStruct(m.shape, F32), jax.ShapeDtypeStruct(zt.shape, F32)],
             in_specs=[vmem] * 4 + [hbm] * len(weights),
-            out_specs=[vmem, vmem],
+            out_specs=[hbm, vmem],
             scratch_shapes=scratch,
             compiler_params=pltpu.CompilerParams(collective_id=0, has_side_effects=True, vmem_limit_bytes=60 * 2**20),
             name='evoformer',
         )(m, zt, mask, rmask.reshape(1, R), *weights)
-        return m_new, z_new.transpose(0, 2, 1)
+        return m_new.astype(BF16), z_new.transpose(0, 2, 1).astype(BF16)
 
     in_specs = (P(('data', 'dap')), P(('data', 'dap')), P('data'), P('data')) + (P(),) * 13
     out_specs = (P(('data', 'dap')), P(('data', 'dap')))

time: 124 us -> 127 us (1.024)
  other arithmetic: 0 us -> 3.2 us
  local copies, waits for them, and re-layouts: 2.85 us -> 0.01 us
  Pallas kernels: 121 us -> 123 us
    convert_element_type x0 -> x2, other arithmetic: none -> 3.2 us  [local_step(): return (m_new.astype(BF16), z_new.transpose(0, 2, 1).astype(BF16))]
    unnamed x4 -> x2, local copies, waits for them, and re-layouts: 2.85 us -> 0.01 us
    pallas_call x1, Pallas kernels: 121 us -> 123 us  [local_step(): pl.pallas_call(functools.partial(step_kernel, cfg), out_shape=[jax.ShapeD...]
where the time goes in v7:
time: 127 us
  Pallas kernels  123 us (97%)
  other arithmetic  3.2 us (3%)
    pallas_call x1, Pallas kernels, local_step(): pl.pallas_call(functools.partial(step_kernel, cfg), out_shape=[jax.ShapeD...  123 us
    convert_element_type x2, other arithmetic, local_step(): return (m_new.astype(BF16), z_new.transpose(0, 2, 1).astype(BF16))  3.2 us

profile of v7, /device:TPU:97, one launch (start us, length us, event | category | flops | bytes accessed | tf_op | source)
XLA Modules:
  0.0 126.6 jit_solution(9934831019342084764)
XLA Ops:
  0.6 122.7 %evoformer.1 = (f32[8,128,384]{2,1,0:T(8,128)}, f32[4,288,128]{2,1,0:T(8,128)}) custom-call(bf16[8,128,384]{2,1,0:T(8,128)(2,1)} %refs_0_.1, bf16[4,288,128]{2,1,0:T(8,128)(2,1)} %bitcast.40, s32[256,128]{1,0:T(8,128)} %refs_2_.1, s32[1,128]{1,0:T(1,128)} %bitcast.45, bf16[12,2,288]{2,1,0:T(2,128)(2,1)} %bitcast.42, bf16[2,1536,384]{2,1,0:T(8,128)(2,1)} %bitcast.31, ...), custom_call_target="tpu_custom_call" | custom-call | tf_op jit(solution)/shard_map/evoformer/pallas_call | solution.py:548
  123.4 0.0 copy-start
  123.4 2.4 %convert_element_type.9 = bf16[8,128,384]{2,1,0:T(8,128)(2,1)} convert(f32[8,128,384]{2,1,0:T(8,128)} %get-tuple-element.4) | non-fusion elementwise | flops 393216 | bytes 2359296 | tf_op jit(solution)/shard_map/convert_element_type | solution.py:557
  125.8 0.0 copy-done
  125.8 0.8 convert_bitcast_fusion
Async XLA Ops:
  123.4 2.5 %copy-start = (f32[4,288,128]{2,1,0:T(8,128)S(1)}, f32[4,288,128]{2,1,0:T(8,128)}, u32[]{:S(2)}) copy-start(f32[4,288,128]{2,1,0:T(8,128)} %get-tuple-element.5) | copy-start | bytes 1769476

commit v8 on v6

--- a/solution.py
+++ b/solution.py
@@ -42,7 +42,7 @@
 
 def softmax_cols(t):
     e = jnp.exp2(t - jnp.max(t, axis=0, keepdims=True))
-    return (e * (1.0 / jnp.sum(e, axis=0, keepdims=True))).astype(BF16)
+    return e.astype(BF16), 1.0 / jnp.sum(e, axis=0, keepdims=True)
 
 
 EXCHANGES = ('b1', 'm1', 'c', 's1', 'z1', 'e1', 'b2', 'a', 'm2', 'e2', 'z2', 's2')
@@ -204,7 +204,8 @@
                 if h + 1 < HT:
                     ahead = logits(h + 1)
                 t = jnp.where(rmaskt[...] > 0, t, NEG)
-                o = mm(part(2, h), softmax_cols(t))
+                e, inverse = softmax_cols(t)
+                o = mm(part(2, h), e) * inverse
                 gpair[u, h * DP:(h + 1) * DP, :] = (o * jax.nn.sigmoid(part(3, h).astype(F32))).astype(BF16)
             dst[i] = (zref[i].astype(F32) + mm(wo, gpair[u])).astype(BF16)
 
@@ -300,7 +301,8 @@
                 if bias is not None:
                     t = t + bias[h]
                 t = jnp.where(mask > 0, t, NEG)
-                o = mm(qvg[p, WM + h * D:WM + (h + 1) * D, keys], softmax_cols(t))
+                e, inverse = softmax_cols(t)
+                o = mm(qvg[p, WM + h * D:WM + (h + 1) * D, keys], e) * inverse
                 g = qvg[p, 2 * WM + h * D:2 * WM + (h + 1) * D, q:q + 128].astype(F32)
                 gbuf[h * D:(h + 1) * D, q:q + 128] = (o * jax.nn.sigmoid(g)).astype(BF16)
 

time: 124 us -> 122 us (0.984)
  Pallas kernels: 121 us -> 118 us
    pallas_call x1, Pallas kernels: 121 us -> 118 us  [local_step(): pl.pallas_call(functools.partial(step_kernel, cfg), out_shape=[jax.ShapeD...]
where the time goes in v8:
time: 122 us
  Pallas kernels  118 us (97%)
  local copies, waits for them, and re-layouts  2.85 us (2%)
    pallas_call x1, Pallas kernels, local_step(): pl.pallas_call(functools.partial(step_kernel, cfg), out_shape=[jax.ShapeD...  118 us
    unnamed x4, local copies, waits for them, and re-layouts  2.85 us

profile of v8, /device:TPU:97, one launch (start us, length us, event | category | flops | bytes accessed | tf_op | source)
XLA Modules:
  0.0 122.0 jit_solution(11046638134746166842)
XLA Ops:
  0.6 118.5 %evoformer.1 = (bf16[8,128,384]{2,1,0:T(8,128)(2,1)}, bf16[4,288,128]{2,1,0:T(8,128)(2,1)}) custom-call(bf16[8,128,384]{2,1,0:T(8,128)(2,1)} %refs_0_.1, bf16[4,288,128]{2,1,0:T(8,128)(2,1)} %bitcast.39, s32[256,128]{1,0:T(8,128)} %refs_2_.1, s32[1,128]{1,0:T(1,128)} %bitcast.45, bf16[12,2,288]{2,1,0:T(2,128)(2,1)} %bitcast.42, ...), custom_call_target="tpu_custom_call" | custom-call | tf_op jit(solution)/shard_map/evoformer/pallas_call | solution.py:540
  119.1 0.0 copy-start
  119.1 2.1 %copy.21 = bf16[8,128,384]{2,1,0:T(8,128)(2,1)} copy(bf16[8,128,384]{2,1,0:T(8,128)(2,1)} %get-tuple-element.8) | data formatting | bytes 1572864
  121.3 0.0 copy-done
  121.3 0.7 copy.22
Async XLA Ops:
  119.1 2.1 %copy-start = (bf16[4,288,128]{2,1,0:T(8,128)(2,1)S(1)}, bf16[4,288,128]{2,1,0:T(8,128)(2,1)}, u32[]{:S(2)}) copy-start(bf16[4,288,128]{2,1,0:T(8,128)(2,1)} %get-tuple-element.5) | copy-start | bytes 884740

commit v9 on v8

--- a/solution.py
+++ b/solution.py
@@ -60,7 +60,7 @@
     side = math.isqrt(n // 2)
     chunk = rl * OP // 2
     it = iter(refs)
-    (m_ref, z_ref, mask_ref, rmask_ref, wb_hbm, wr_hbm, wro_hbm, wc_hbm, wco_hbm, wpi_hbm, wpo_hbm,
+    (m_hbm, z_hbm, mask_hbm, rmask_hbm, wb_hbm, wr_hbm, wro_hbm, wc_hbm, wco_hbm, wpi_hbm, wpo_hbm,
      wsb_hbm, ws_hbm, wso_hbm, web_hbm, we_hbm, weo_hbm) = [next(it) for _ in range(17)]
     m_out, z_out = next(it), next(it)
     wb, wr, wro, wc, wco, wpi, wpo, wsb, ws, wso, web, we, weo = weights = [next(it) for _ in range(13)]
@@ -77,6 +77,11 @@
         send[name] = next(it)
         recv[name] = next(it)
     send_sem, recv_sem, w_sem = next(it), next(it), next(it)
+    m_ref, z_ref, mask_ref, rmask_ref, mfinal, in_sem = [next(it) for _ in range(6)]
+    inputs = [pltpu.make_async_copy(src, dst, in_sem.at[i]) for i, (src, dst) in enumerate(
+        [(mask_hbm, mask_ref), (rmask_hbm, rmask_ref), (z_hbm, z_ref), (m_hbm, m_ref)])]
+    for load in inputs:
+        load.start()
     hbm = [wb_hbm, wr_hbm, wro_hbm, wc_hbm, wco_hbm, wpi_hbm, wpo_hbm, wsb_hbm, ws_hbm, wso_hbm, web_hbm, we_hbm, weo_hbm]
     loads = [pltpu.make_async_copy(src, dst, w_sem.at[i]) for i, (src, dst) in enumerate(zip(hbm, weights))]
     for load in loads:
@@ -103,9 +108,8 @@
         pltpu.make_async_copy(like, like, sems.at[FLOWS.index(flow)]).wait()
 
     def push(flow, src, dst, scatter):
-        @pl.loop(1, n)
-        def _(k):
-            peer = lax.rem(me + k * STRIDE, n)
+        for k in range(1, n):
+            peer = lax.rem(me + k * STRIDE % n, n)
             remote(flow, src.at[peer] if scatter else src, dst.at[me], {'dap': peer}).start()
         dst[me] = src[me] if scatter else src[...]
 
@@ -339,6 +343,8 @@
             c_dst[at, :] = half[OP:2 * OP]
             after(i)
 
+    for load in inputs:
+        load.wait()
     maskf = mask_ref[...].astype(F32).astype(BF16)
     mcolmask[...] = maskf
     seqmask[...] = mask_ref[pl.ds(pl.multiple_of(me * sl, sl), sl), :].astype(F32)
@@ -470,7 +476,9 @@
     bias_block('s2', wsb[1], HT)
     arrived('b2')
     bias_build('b2', H, 8, bias_f, False)
-    row_attend(mrow, wro.at[1], bias_f, m_out, 0, sl // 2)
+    row_attend(mrow, wro.at[1], bias_f, mfinal, 0, sl // 2)
+    store = pltpu.make_async_copy(mfinal, m_out, in_sem.at[0])
+    store.start()
     arrived('z2')
     pair_receive('z2')
     pair_norm(zb)
@@ -478,6 +486,7 @@
     arrived('s2')
     bias_build('s2', HT, 4, biast_f, False)
     pair_attend(zb, wsot[1], z_out)
+    store.wait()
     for flow in FLOWS:
         wait_for(flow, send_sem, like(flow))
 
@@ -534,14 +543,15 @@
             else:
                 scratch += [vm((n,) + shape if name[0] == 'z' else shape), vm((n,) + shape)]
         scratch += [pltpu.SemaphoreType.DMA((len(FLOWS),)), pltpu.SemaphoreType.DMA((len(FLOWS),)), pltpu.SemaphoreType.DMA((len(weights),))]
+        scratch += [vm(m.shape), vm(zt.shape), vm(mask.shape, mask.dtype), vm((1, R), rmask.dtype), vm(m.shape), pltpu.SemaphoreType.DMA((4,))]
         cfg = (n, sl, rl, S, R, CM, CZ, H, D, HT, DT, OP, HP)
         vmem = pl.BlockSpec(memory_space=pltpu.VMEM)
         hbm = pl.BlockSpec(memory_space=pl.ANY)
         m_new, z_new = pl.pallas_call(
             functools.partial(step_kernel, cfg),
             out_shape=[jax.ShapeDtypeStruct(m.shape, BF16), jax.ShapeDtypeStruct(zt.shape, BF16)],
-            in_specs=[vmem] * 4 + [hbm] * len(weights),
-            out_specs=[vmem, vmem],
+            in_specs=[hbm] * (4 + len(weights)),
+            out_specs=[hbm, vmem],
             scratch_shapes=scratch,
             compiler_params=pltpu.CompilerParams(collective_id=0, has_side_effects=True, vmem_limit_bytes=60 * 2**20),
             name='evoformer',

time: 122 us -> 122 us (level)
  no operation moved by 1% of the time
where the time goes in v9:
time: 122 us
  Pallas kernels  118 us (97%)
  local copies, waits for them, and re-layouts  2.85 us (2%)
    pallas_call x1, Pallas kernels, local_step(): pl.pallas_call(functools.partial(step_kernel, cfg), out_shape=[jax.ShapeD...  118 us
    unnamed x4, local copies, waits for them, and re-layouts  2.85 us

profile of v9, /device:TPU:97, one launch (start us, length us, event | category | flops | bytes accessed | tf_op | source)
XLA Modules:
  0.0 121.7 jit_solution(3677149466261419422)
XLA Ops:
  0.6 118.2 %evoformer.1 = (bf16[8,128,384]{2,1,0:T(8,128)(2,1)}, bf16[4,288,128]{2,1,0:T(8,128)(2,1)}) custom-call(bf16[8,128,384]{2,1,0:T(8,128)(2,1)} %refs_0_.1, bf16[4,288,128]{2,1,0:T(8,128)(2,1)} %bitcast.39, s32[256,128]{1,0:T(8,128)} %refs_2_.1, s32[1,128]{1,0:T(1,128)} %bitcast.45, bf16[12,2,288]{2,1,0:T(2,128)(2,1)} %bitcast.42, ...), custom_call_target="tpu_custom_call" | custom-call | tf_op jit(solution)/shard_map/evoformer/pallas_call | solution.py:550
  118.8 0.0 copy-start
  118.9 2.1 %copy.21 = bf16[8,128,384]{2,1,0:T(8,128)(2,1)} copy(bf16[8,128,384]{2,1,0:T(8,128)(2,1)} %get-tuple-element.8) | data formatting | bytes 1572864
  121.0 0.0 copy-done
  121.0 0.7 copy.22
Async XLA Ops:
  118.8 2.1 %copy-start = (bf16[4,288,128]{2,1,0:T(8,128)(2,1)S(1)}, bf16[4,288,128]{2,1,0:T(8,128)(2,1)}, u32[]{:S(2)}) copy-start(bf16[4,288,128]{2,1,0:T(8,128)(2,1)} %get-tuple-element.5) | copy-start | bytes 884740

commit v10 on v9

--- a/solution.py
+++ b/solution.py
@@ -108,8 +108,9 @@
         pltpu.make_async_copy(like, like, sems.at[FLOWS.index(flow)]).wait()
 
     def push(flow, src, dst, scatter):
-        for k in range(1, n):
-            peer = lax.rem(me + k * STRIDE % n, n)
+        @pl.loop(1, n)
+        def _(k):
+            peer = lax.rem(me + k * STRIDE, n)
             remote(flow, src.at[peer] if scatter else src, dst.at[me], {'dap': peer}).start()
         dst[me] = src[me] if scatter else src[...]
 

time: 122 us -> 121 us (level)
  no operation moved by 1% of the time
where the time goes in v10:
time: 121 us
  Pallas kernels  118 us (98%)
  local copies, waits for them, and re-layouts  2.85 us (2%)
    pallas_call x1, Pallas kernels, local_step(): pl.pallas_call(functools.partial(step_kernel, cfg), out_shape=[jax.ShapeD...  118 us
    unnamed x4, local copies, waits for them, and re-layouts  2.85 us

profile of v10, /device:TPU:97, one launch (start us, length us, event | category | flops | bytes accessed | tf_op | source)
XLA Modules:
  0.0 121.2 jit_solution(1662343615872127720)
XLA Ops:
  0.6 117.7 %evoformer.1 = (bf16[8,128,384]{2,1,0:T(8,128)(2,1)}, bf16[4,288,128]{2,1,0:T(8,128)(2,1)}) custom-call(bf16[8,128,384]{2,1,0:T(8,128)(2,1)} %refs_0_.1, bf16[4,288,128]{2,1,0:T(8,128)(2,1)} %bitcast.39, s32[256,128]{1,0:T(8,128)} %refs_2_.1, s32[1,128]{1,0:T(1,128)} %bitcast.45, bf16[12,2,288]{2,1,0:T(2,128)(2,1)} %bitcast.42, ...), custom_call_target="tpu_custom_call" | custom-call | tf_op jit(solution)/shard_map/evoformer/pallas_call | solution.py:551
  118.3 0.0 copy-start
  118.3 2.1 %copy.21 = bf16[8,128,384]{2,1,0:T(8,128)(2,1)} copy(bf16[8,128,384]{2,1,0:T(8,128)(2,1)} %get-tuple-element.8) | data formatting | bytes 1572864
  120.5 0.0 copy-done
  120.5 0.7 copy.22
Async XLA Ops:
  118.3 2.1 %copy-start = (bf16[4,288,128]{2,1,0:T(8,128)(2,1)S(1)}, bf16[4,288,128]{2,1,0:T(8,128)(2,1)}, u32[]{:S(2)}) copy-start(bf16[4,288,128]{2,1,0:T(8,128)(2,1)} %get-tuple-element.5) | copy-start | bytes 884740

commit v11 on v10

--- a/solution.py
+++ b/solution.py
@@ -444,12 +444,12 @@
     pair_norm(zb)
     bias_block('e1', web[0], HT)
     share('a')
+    send_cols(1)
     arrived('z1')
     pair_receive('z1')
     pair_norm(zb)
     pair_project(wep[0])
     arrived('e1')
-    send_cols(1)
     bias_build('e1', HT, 4, biast_f, False)
     pair_attend(zb, weot[0], zb)
 

time: 121 us -> 123 us (1.017)
    pallas_call x1, Pallas kernels: 118 us -> 119 us  [local_step(): pl.pallas_call(functools.partial(step_kernel, cfg), out_shape=[jax.ShapeD...]
where the time goes in v11:
time: 123 us
  Pallas kernels  119 us (97%)
  local copies, waits for them, and re-layouts  2.85 us (2%)
    pallas_call x1, Pallas kernels, local_step(): pl.pallas_call(functools.partial(step_kernel, cfg), out_shape=[jax.ShapeD...  119 us
    unnamed x4, local copies, waits for them, and re-layouts  2.85 us

profile of v11, /device:TPU:97, one launch (start us, length us, event | category | flops | bytes accessed | tf_op | source)
XLA Modules:
  0.0 122.9 jit_solution(17989786893203587283)
XLA Ops:
  0.6 119.4 %evoformer.1 = (bf16[8,128,384]{2,1,0:T(8,128)(2,1)}, bf16[4,288,128]{2,1,0:T(8,128)(2,1)}) custom-call(bf16[8,128,384]{2,1,0:T(8,128)(2,1)} %refs_0_.1, bf16[4,288,128]{2,1,0:T(8,128)(2,1)} %bitcast.39, s32[256,128]{1,0:T(8,128)} %refs_2_.1, s32[1,128]{1,0:T(1,128)} %bitcast.45, bf16[12,2,288]{2,1,0:T(2,128)(2,1)} %bitcast.42, ...), custom_call_target="tpu_custom_call" | custom-call | tf_op jit(solution)/shard_map/evoformer/pallas_call | solution.py:551
  120.1 0.0 copy-start
  120.1 2.1 %copy.21 = bf16[8,128,384]{2,1,0:T(8,128)(2,1)} copy(bf16[8,128,384]{2,1,0:T(8,128)(2,1)} %get-tuple-element.8) | data formatting | bytes 1572864
  122.2 0.0 copy-done
  122.2 0.7 copy.22
Async XLA Ops:
  120.1 2.1 %copy-start = (bf16[4,288,128]{2,1,0:T(8,128)(2,1)S(1)}, bf16[4,288,128]{2,1,0:T(8,128)(2,1)}, u32[]{:S(2)}) copy-start(bf16[4,288,128]{2,1,0:T(8,128)(2,1)} %get-tuple-element.5) | copy-start | bytes 884740
